TPU v7x, 32 devices: a whole 2x2x4 slice. The times are simulated.
32 devices in a mesh: dom: 32 (over z, y, x, core).
Axes of the slice: x: 2, y: 2, z: 4, core: 2. Of those that a mesh axis runs over, the one named last changes fastest.
Arguments:
- features: bfloat16 [524288, 256], P('dom'), may hold values from -48 to 48, as said below
- w_first: bfloat16 [1280, 256], replicated, may hold values from -0.15625 to 0.15625
- w_second: bfloat16 [1280, 256], replicated, may hold values from -0.15625 to 0.15625
- seed_owner: int32 [9216, 1], P('dom'), may hold values from 0 to 31; in each aligned block of 288 rows (0 to 287, 288 to 575, ...) at most 18 rows name the same one
- seed_row: int32 [9216], P('dom'), may hold values from 0 to 16383
- hop1_owner: int32 [36864, 1], P('dom'), may hold values from 0 to 31; in each aligned block of 1152 rows (0 to 1151, 1152 to 2303, ...) at most 72 rows name the same one
- hop1_row: int32 [36864], P('dom'), may hold values from 0 to 16383
- hop1_rel: int32 [36864], P('dom'), may hold values from 0 to 3
- hop2_owner: int32 [73728, 1], P('dom'), may hold values from 0 to 31; in each aligned block of 2304 rows (0 to 2303, 2304 to 4607, ...) at most 144 rows name the same one
- hop2_row: int32 [73728], P('dom'), may hold values from 0 to 16383
- hop2_rel: int32 [73728], P('dom'), may hold values from 0 to 3
- edge_mask: int32 [4096], P('dom'), may hold values 0 or 1
Outputs:
- edge_loss: float32 [4096], P('dom')
- mean_loss: float32 [], replicated
Inputs may be any that keep to these rules, and one draw needn't show every extreme that they name: `features`: standard normal entries; in some draws each row is scaled by a factor up to 10. `seed_owner`: among the rows of one device no owner is named by more than 18 rows; some owner is named by exactly 18 in every draw. `hop1_owner`: among the rows of one device no owner is named by more than 72 rows; some owner is named by exactly 72 in every draw. `hop2_owner`: among the rows of one device no owner is named by more than 144 rows; some owner is named by exactly 144 in every draw.
All inputs are finite; a program needn't handle non-finite values. No bound on the sum of `edge_mask` on one device may be relied on, other than what follows from the above.
Results may differ from a plain program's by a relative error of at most 0.002.
Values may be sent and summed in bfloat16 or wider, within the bound.
No kernel may reach another device: no remote copies, remote signals or barrier semaphores. Data moves between devices by JAX's collectives and lax.ppermute only.
A program may use at most 64 MiB of HBM per device.

v0:
```python
import jax
import jax.numpy as jnp
from jax import lax
from jax.sharding import PartitionSpec as P

R = 4
BLOCK = 128
NEG = 32
FAN1 = 4
FAN2 = 2


def bucket_rows(owner, rows, devices, capacity):
    owners = owner[:, 0]
    length = owners.shape[0]
    onehot = (owners[:, None] == jnp.arange(devices, dtype=jnp.int32)[None, :]).astype(jnp.bfloat16)
    counter = jnp.arange(length, dtype=jnp.int32)
    earlier = (counter[:, None] > counter[None, :]).astype(jnp.bfloat16)
    prior = jnp.dot(earlier, onehot, preferred_element_type=jnp.float32)
    position = jnp.sum(prior * onehot.astype(jnp.float32), axis=1).astype(jnp.int32)
    slot_index = owners * capacity + position
    slot_hot = (
        slot_index[:, None] == jnp.arange(devices * capacity, dtype=jnp.int32)[None, :]
    ).astype(jnp.bfloat16)
    halves = jnp.stack([rows // 128, rows % 128], axis=1).astype(jnp.bfloat16)
    placed = lax.dot_general(
        slot_hot, halves, (((0,), (0,)), ((), ())), preferred_element_type=jnp.float32
    )
    requests = (placed[:, 0] * 128.0 + placed[:, 1]).astype(jnp.int32)
    return (slot_index, requests.reshape(devices, capacity))


def unpack_rows(returned, slot_index):
    return returned[slot_index]


def fetch_apart(owner, rows, features, devices):
    capacity = (2 * owner.shape[0] + devices - 1) // devices
    slot_index, requests = bucket_rows(owner, rows, devices, capacity)
    arrived = lax.all_to_all(requests, "dom", split_axis=0, concat_axis=0, tiled=True)
    located = features[arrived.reshape(-1)].reshape(devices, capacity, features.shape[1])
    returned = lax.all_to_all(located, "dom", split_axis=0, concat_axis=0, tiled=True)
    return unpack_rows(returned.reshape(devices * capacity, features.shape[1]), slot_index)


def rgcn_layer(self_rows, neighbours, relations, weights):
    width = self_rows.shape[1]
    onehot = (relations[..., None] == jnp.arange(R, dtype=jnp.int32)).astype(jnp.float32)
    tallies = jnp.maximum(jnp.sum(onehot, axis=1), 1.0)
    shares = onehot / tallies[:, None, :]
    merged = shares[:, 0, :, None] * neighbours[:, 0, None, :].astype(jnp.float32)
    for column in range(1, neighbours.shape[1]):
        merged = merged + shares[:, column, :, None] * neighbours[:, column, None, :].astype(
            jnp.float32
        )
    merged = merged.astype(jnp.bfloat16).reshape(self_rows.shape[0], R * width)
    inputs = jnp.concatenate([self_rows, merged], axis=1)
    return jnp.dot(inputs, weights, preferred_element_type=jnp.float32)


def shards(
    features,
    w_first,
    w_second,
    seed_owner,
    seed_row,
    hop1_owner,
    hop1_row,
    hop1_rel,
    hop2_owner,
    hop2_row,
    hop2_rel,
    edge_mask,
):
    devices = lax.axis_size("dom")
    width = features.shape[1]
    seed_count = seed_row.shape[0]
    first_count = hop1_row.shape[0]
    positives = edge_mask.shape[0]
    blocks = positives // BLOCK
    x_hop2 = fetch_apart(hop2_owner, hop2_row, features, devices)
    x_hop1 = fetch_apart(hop1_owner, hop1_row, features, devices)
    x_seed = fetch_apart(seed_owner, seed_row, features, devices)
    first_hop = jax.nn.relu(
        rgcn_layer(
            x_hop1,
            x_hop2.reshape(first_count, FAN2, width),
            hop2_rel.reshape(first_count, FAN2),
            w_first,
        )
    ).astype(jnp.bfloat16)
    first_seed = jax.nn.relu(
        rgcn_layer(
            x_seed,
            x_hop1.reshape(seed_count, FAN1, width),
            hop1_rel.reshape(seed_count, FAN1),
            w_first,
        )
    ).astype(jnp.bfloat16)
    second = rgcn_layer(
        first_seed,
        first_hop.reshape(seed_count, FAN1, width),
        hop1_rel.reshape(seed_count, FAN1),
        w_second,
    )
    sources = second[:positives]
    targets = second[positives : 2 * positives]
    negatives = second[2 * positives :].reshape(blocks, NEG, width)
    positive = jnp.sum(sources * targets, axis=1)
    negative = jnp.einsum(
        "bef,bqf->beq",
        sources.reshape(blocks, BLOCK, width),
        negatives,
        precision=lax.Precision.HIGHEST,
    ).reshape(positives, NEG)
    scores = jnp.concatenate([positive[:, None], negative], axis=1)
    top_score = jnp.max(scores, axis=1, keepdims=True)
    edge_loss = top_score[:, 0] + jnp.log(jnp.sum(jnp.exp(scores - top_score), axis=1)) - positive
    weights = edge_mask.astype(jnp.float32)
    loss_total, edge_total = lax.psum((jnp.sum(weights * edge_loss), jnp.sum(weights)), "dom")
    mean_loss = loss_total / jnp.maximum(edge_total, 1.0)
    return (edge_loss, mean_loss)


def solution(mesh):
    placed = (
        P("dom", None),
        P(),
        P(),
        P("dom", None),
        P("dom"),
        P("dom", None),
        P("dom"),
        P("dom"),
        P("dom", None),
        P("dom"),
        P("dom"),
        P("dom"),
    )
    return jax.shard_map(
        shards, mesh=mesh, in_specs=placed, out_specs=(P("dom"), P()), check_vma=False
    )
```

profile of v0, /device:TPU:0, one launch (start us, length us, event | category | flops | bytes accessed | tf_op | source)
XLA Modules:
  0.0 227.9 jit_solution(11600786799563126268)
XLA Ops:
  4.1 7.3 %all-to-all-start = ((s32[32,1,18]{2,1,0:T(1,128)}), s32[32,1,18]{2,1,0:T(1,128)S(1)}, u32[]{:S(2)}, u32[]{:S(2)}) async-start(s32[32,1,18]{2,1,0:T(1,128)} %bitcast), calls=%async_computation | async-start | bytes 32768 | tf_op jit(solution)/shard_map/all_to_all | solution.py:40
  12.2 1.9 fusion.19
  14.2 7.4 %fusion = f32[4608,2]{0,1:T(2,128)S(1)} fusion(s32[2304]{0:T(1024)S(1)} %get-tuple-element.3, bf16[2304,1]{0,1:T(2,128)(2,1)S(1)} %stack.43, bf16[2304,1]{0,1:T(2,128)(2,1)S(1)} %stack.42), kind=kOutput, calls=%fused_computation.7 | convolution fusion | flops 53102592 | bytes 55296 | tf_op jit(solution)/shard_map/dot_general | solution.py:26
  22.5 2.0 fusion.3
  25.9 6.0 %all-to-all-start.2 = ((s32[32,1,72]{2,1,0:T(1,128)}), s32[32,1,72]{2,1,0:T(1,128)S(1)}, u32[]{:S(2)}, u32[]{:S(2)}) async-start(s32[32,1,72]{2,1,0:T(1,128)} %bitcast.2), calls=%async_computation.2 | async-start | bytes 32768 | tf_op jit(solution)/shard_map/all_to_all | solution.py:40
  33.3 5.7 %all-to-all-done.2 = s32[32,1,72]{2,1,0:T(1,128)S(1)} async-done(((s32[32,1,72]{2,1,0:T(1,128)}), s32[32,1,72]{2,1,0:T(1,128)S(1)}, u32[]{:S(2)}, u32[]{:S(2)}) %all-to-all-start.2) | async-done | bytes 9248 | tf_op jit(solution)/shard_map/all_to_all | solution.py:40
  38.9 2.6 %all-to-all-start.4 = ((s32[32,1,144]{2,1,0:T(1,128)}), s32[32,1,144]{2,1,0:T(1,128)S(1)}, u32[]{:S(2)}, u32[]{:S(2)}) async-start(s32[32,1,144]{2,1,0:T(1,128)} %convert_element_type.173), calls=%async_computation.4 | async-start | bytes 65536 | tf_op jit(solution)/shard_map/all_to_all | solution.py:40
  41.5 6.6 %gather_fusion = bf16[576,256]{1,0:T(8,128)(2,1)S(1)} fusion(bf16[16384,256]{1,0:T(8,128)(2,1)} %param.12, s32[1024]{0:T(1024)S(1)} %pad_clamp_fusion.5), kind=kCustom, calls=%fused_computation | custom fusion | bytes 592128 | tf_op jit(solution)/shard_map/gather | solution.py:41
  49.0 5.8 %all-to-all-start.1 = ((bf16[32,18,256]{2,1,0:T(8,128)(2,1)}), bf16[32,18,256]{2,1,0:T(8,128)(2,1)S(1)}, u32[]{:S(2)}, u32[]{:S(2)}) async-start(bf16[32,18,256]{2,1,0:T(8,128)(2,1)} %reshape.323), calls=%async_computation.1 | async-start | bytes 786432 | tf_op jit(solution)/shard_map/all_to_all | solution.py:42
  55.7 10.7 %gather_fusion.2 = bf16[2304,256]{1,0:T(8,128)(2,1)} fusion(bf16[16384,256]{1,0:T(8,128)(2,1)} %param.12, s32[3072]{0:T(1024)S(1)} %pad_clamp_fusion.2), kind=kCustom, calls=%fused_computation.2 | custom fusion | bytes 2368512 | tf_op jit(solution)/shard_map/gather | solution.py:41
  68.8 4.1 %all-to-all-start.3 = ((bf16[32,72,256]{2,1,0:T(8,128)(2,1)}), bf16[32,72,256]{2,1,0:T(8,128)(2,1)S(1)}, u32[]{:S(2)}, u32[]{:S(2)}) async-start(bf16[32,72,256]{2,1,0:T(8,128)(2,1)} %bitcast.3), calls=%async_computation.3 | async-start | bytes 2359296 | tf_op jit(solution)/shard_map/all_to_all | solution.py:42
  73.2 15.8 %gather_fusion.4 = bf16[4608,256]{1,0:T(8,128)(2,1)} fusion(bf16[16384,256]{1,0:T(8,128)(2,1)} %param.12, s32[5120]{0:T(1024)S(1)} %pad_clamp_fusion), kind=kCustom, calls=%fused_computation.4 | custom fusion | bytes 4737024 | tf_op jit(solution)/shard_map/gather | solution.py:41
  89.1 12.9 %all-to-all-done.3 = bf16[32,72,256]{2,1,0:T(8,128)(2,1)S(1)} async-done(((bf16[32,72,256]{2,1,0:T(8,128)(2,1)}), bf16[32,72,256]{2,1,0:T(8,128)(2,1)S(1)}, u32[]{:S(2)}, u32[]{:S(2)}) %all-to-all-start.3) | async-done | bytes 1179680 | tf_op jit(solution)/shard_map/all_to_all | solution.py:42
  103.0 3.6 %all-to-all-start.5 = ((bf16[32,144,256]{2,1,0:T(8,128)(2,1)}), bf16[32,144,256]{2,1,0:T(8,128)(2,1)S(1)}, u32[]{:S(2)}, u32[]{:S(2)}) async-start(bf16[32,144,256]{2,1,0:T(8,128)(2,1)} %bitcast.54), calls=%async_computation.5 | async-start | bytes 4718592 | tf_op jit(solution)/shard_map/all_to_all | solution.py:42
  115.5 2.5 %gather_fusion.1 = bf16[288,256]{1,0:T(8,128)(2,1)} fusion(bf16[576,256]{1,0:T(8,128)(2,1)S(1)} %reshape.324, s32[1024]{0:T(1024)S(1)} %pad_clamp_fusion.4), kind=kCustom, calls=%fused_computation.1 | custom fusion | bytes 296064 | tf_op jit(solution)/shard_map/gather | solution.py:34
  118.1 5.4 %gather_fusion.3 = bf16[1152,256]{1,0:T(8,128)(2,1)} fusion(bf16[2304,256]{1,0:T(8,128)(2,1)} %bitcast.53, s32[2048]{0:T(1024)S(1)} %pad_clamp_fusion.3), kind=kCustom, calls=%fused_computation.3 | custom fusion | bytes 1184256 | tf_op jit(solution)/shard_map/gather | solution.py:34
  123.4 2.3 reshape.328
  125.7 2.9 %slice_convert_fusion.9 = (f32[288,1,256]{2,1,0:T(1,128)S(1)}, f32[288,1,256]{2,1,0:T(1,128)S(1)}, f32[288,1,256]{2,1,0:T(1,128)S(1)}, f32[288,1,256]{2,1,0:T(1,128)S(1)}) fusion(bf16[288,4,256]{2,1,0:T(4,128)(2,1)} %reshape.328), kind=kLoop, calls=%fused_computation.55 | loop fusion | flops 294912 | bytes 1769472 | tf_op jit(solution)/shard_map/mul | solution.py:51
  130.3 30.7 %all-to-all-done.5 = bf16[32,144,256]{2,1,0:T(8,128)(2,1)S(1)} async-done(((bf16[32,144,256]{2,1,0:T(8,128)(2,1)}), bf16[32,144,256]{2,1,0:T(8,128)(2,1)S(1)}, u32[]{:S(2)}, u32[]{:S(2)}) %all-to-all-start.5) | async-done | bytes 2359328 | tf_op jit(solution)/shard_map/all_to_all | solution.py:42
  161.0 7.4 %gather_fusion.5 = bf16[2304,256]{1,0:T(8,128)(2,1)} fusion(bf16[4608,256]{1,0:T(8,128)(2,1)S(1)} %bitcast.52, s32[3072]{0:T(1024)S(1)} %pad_clamp_fusion.1), kind=kCustom, calls=%fused_computation.5 | custom fusion | bytes 2368512 | tf_op jit(solution)/shard_map/gather | solution.py:34
  168.4 2.9 %reshape.332 = bf16[1152,2,256]{2,1,0:T(2,128)(2,1)S(1)} reshape(bf16[2304,256]{1,0:T(8,128)(2,1)} %gather_fusion.5) | data formatting | bytes 2359296 | tf_op jit(solution)/shard_map/reshape | solution.py:87
  174.2 3.3 %add_convert_fusion = bf16[1152,4,256]{2,1,0:T(4,128)(2,1)S(1)} fusion(f32[1152,256]{1,0:T(8,128)S(1)} %get-tuple-element.43, f32[1152,4]{1,0:T(8,128)S(1)} %copy-done.3, f32[1152,256]{1,0:T(8,128)S(1)} %get-tuple-element.44, f32[1152,4]{1,0:T(8,128)S(1)} %copy-done.2), kind=kLoop, calls=%fused_computation.16 | loop fusion | flops 4718592 | bytes 4755456 | tf_op jit(solution)/shard_map/convert_element_type | solution.py:56
  181.8 2.0 add_convert_fusion.2
  187.2 38.4 %all-reduce = (f32[]{:T(128)}, f32[]{:T(128)}) all-reduce(f32[]{:T(128)} %get-tuple-element.9, f32[]{:T(128)} %get-tuple-element.8), channel_id=1, replica_groups=mesh['dom'=32] {'dom'}, use_global_device_ids=true, to_apply=%region_9.10 | all-reduce | flops 2 | bytes 16 | tf_op jit(solution)/shard_map/psum | solution.py:120
  (129 shorter events, 33.9 us)
Async XLA Ops:
  0.6 177.5 %copy-start = (bf16[1280,256]{1,0:T(8,128)(2,1)S(1)}, bf16[1280,256]{1,0:T(8,128)(2,1)}, u32[]{:S(2)}) copy-start(bf16[1280,256]{1,0:T(8,128)(2,1)} %param.13) | copy-start | bytes 1966084
  4.1 21.8 %all-to-all-start = ((s32[32,1,18]{2,1,0:T(1,128)}), s32[32,1,18]{2,1,0:T(1,128)S(1)}, u32[]{:S(2)}, u32[]{:S(2)}) async-start(s32[32,1,18]{2,1,0:T(1,128)} %bitcast), calls=%async_computation | async-start | bytes 32768 | tf_op jit(solution)/shard_map/all_to_all | solution.py:40
  12.1 1.9 copy-start.13
  12.1 2.0 copy-start.15
  14.2 7.5 %copy-start.14 = (s32[1152,1]{0,1:T(1,128)S(1)}, s32[1152,1]{0,1:T(1,128)}, u32[]{:S(2)}) copy-start(s32[1152,1]{0,1:T(1,128)} %param.17) | copy-start | bytes 13828
  25.9 13.0 %all-to-all-start.2 = ((s32[32,1,72]{2,1,0:T(1,128)}), s32[32,1,72]{2,1,0:T(1,128)S(1)}, u32[]{:S(2)}, u32[]{:S(2)}) async-start(s32[32,1,72]{2,1,0:T(1,128)} %bitcast.2), calls=%async_computation.2 | async-start | bytes 32768 | tf_op jit(solution)/shard_map/all_to_all | solution.py:40
  38.9 10.0 %all-to-all-start.4 = ((s32[32,1,144]{2,1,0:T(1,128)}), s32[32,1,144]{2,1,0:T(1,128)S(1)}, u32[]{:S(2)}, u32[]{:S(2)}) async-start(s32[32,1,144]{2,1,0:T(1,128)} %convert_element_type.173), calls=%async_computation.4 | async-start | bytes 65536 | tf_op jit(solution)/shard_map/all_to_all | solution.py:40
  49.0 19.1 %all-to-all-start.1 = ((bf16[32,18,256]{2,1,0:T(8,128)(2,1)}), bf16[32,18,256]{2,1,0:T(8,128)(2,1)S(1)}, u32[]{:S(2)}, u32[]{:S(2)}) async-start(bf16[32,18,256]{2,1,0:T(8,128)(2,1)} %reshape.323), calls=%async_computation.1 | async-start | bytes 786432 | tf_op jit(solution)/shard_map/all_to_all | solution.py:42
  68.8 33.2 %all-to-all-start.3 = ((bf16[32,72,256]{2,1,0:T(8,128)(2,1)}), bf16[32,72,256]{2,1,0:T(8,128)(2,1)S(1)}, u32[]{:S(2)}, u32[]{:S(2)}) async-start(bf16[32,72,256]{2,1,0:T(8,128)(2,1)} %bitcast.3), calls=%async_computation.3 | async-start | bytes 2359296 | tf_op jit(solution)/shard_map/all_to_all | solution.py:42
  102.0 1.0 copy-start.1
  102.0 4.6 %copy-start.16 = (s32[2304]{0:T(1024)S(1)}, s32[2304]{0:T(1024)}, u32[]{:S(2)}) copy-start(s32[2304]{0:T(1024)} %param.22) | copy-start | bytes 27652
  103.0 58.0 %all-to-all-start.5 = ((bf16[32,144,256]{2,1,0:T(8,128)(2,1)}), bf16[32,144,256]{2,1,0:T(8,128)(2,1)S(1)}, u32[]{:S(2)}, u32[]{:S(2)}) async-start(bf16[32,144,256]{2,1,0:T(8,128)(2,1)} %bitcast.54), calls=%async_computation.5 | async-start | bytes 4718592 | tf_op jit(solution)/shard_map/all_to_all | solution.py:42
  106.6 4.9 %copy-start.17 = (s32[1152]{0:T(1024)S(1)}, s32[1152]{0:T(1024)}, u32[]{:S(2)}) copy-start(s32[1152]{0:T(1024)} %param.19) | copy-start | bytes 13828
  173.0 1.1 copy-start.2
  173.0 1.2 copy-start.3
  177.5 1.1 copy-start.4
  180.5 1.0 copy-start.6
  180.5 1.0 copy-start.7
  180.5 1.1 copy-start.8
  180.6 1.2 copy-start.9
  180.6 1.2 copy-start.10
  180.6 1.2 copy-start.11
  183.8 0.9 copy-start.12
  184.1 1.1 copy-start.20
  (3 other events, 2.4 us)
where the time goes:
time: 229 us; the launch traced here: 228 us
  local copies, waits for them, and re-layouts  74 us (32%)
  waiting for transfers between devices  51 us (22%)
  blocking collectives  38.4 us (17%)
  starting transfers between devices  29.5 us (13%)
  other arithmetic  17 us (7%)
  matrix products  14.3 us (6%)
  between operations  3.68 us (2%)
    all_to_all x3, waiting for transfers between devices, fetch_apart(): lax.all_to_all(located, 'dom', split_axis=0, concat_axis=0, tiled=True)  45.4 us
    psum x1, blocking collectives, shards(): lax.psum((jnp.sum(weights * edge_loss), jnp.sum(weights)), 'dom')  38.4 us
    gather x3, local copies, waits for them, and re-layouts, fetch_apart(): features[arrived.reshape(-1)].reshape(devices, capacity, features.shape[1])  33.1 us
    all_to_all x3, starting transfers between devices, fetch_apart(): lax.all_to_all(requests, 'dom', split_axis=0, concat_axis=0, tiled=True)  15.9 us
    gather x3, local copies, waits for them, and re-layouts, unpack_rows(): return returned[slot_index]  15.3 us
    all_to_all x3, starting transfers between devices, fetch_apart(): lax.all_to_all(located, 'dom', split_axis=0, concat_axis=0, tiled=True)  13.6 us
    dot_general x3, matrix products, bucket_rows(): lax.dot_general(slot_hot, halves, (((0,), (0,)), ((), ())), preferred_ele...  9.68 us
    unnamed x52, local copies, waits for them, and re-layouts  7.83 us
  transfers between devices with their start and end apart: 6, of which 4 were waited for; matrix products, arithmetic and copies ran while one was open for 33% of the time, Pallas kernels for 0%

commit v1 on v0

v1 whole, which is shorter than its diff:
```python
import functools

import jax
import jax.numpy as jnp
from jax import lax
from jax.experimental import pallas as pl
from jax.experimental.pallas import tpu as pltpu
from jax.sharding import PartitionSpec as P

R = 4
BLOCK = 128
NEG = 32
FAN1 = 4
FAN2 = 2
LANES = 128
F32 = jnp.float32
BF16 = jnp.bfloat16
HIGHEST = lax.Precision.HIGHEST


def round_up(value, unit):
    return (value + unit - 1) // unit * unit


def full(memory_space=pltpu.VMEM):
    return pl.BlockSpec(memory_space=memory_space)


def bucket_kernel(offsets, stride, counts, *refs):
    kinds = len(counts)
    owner_refs, row_refs = refs[:kinds], refs[kinds : 2 * kinds]
    request_ref, slot_ref = refs[2 * kinds :]
    devices, _, width = request_ref.shape
    device = lax.broadcasted_iota(jnp.int32, (devices, LANES), 0)
    before = lax.broadcasted_iota(jnp.int32, (LANES, 2 * LANES), 0)
    lane = lax.broadcasted_iota(jnp.int32, (LANES, 2 * LANES), 1)
    earlier = jnp.where(before < lane, 1.0, 0.0).astype(BF16)
    place = lax.broadcasted_iota(jnp.int32, (width, LANES), 0)
    total = jnp.zeros((2 * devices, width), F32)
    block = 0
    for kind, count in enumerate(counts):
        carried = jnp.zeros((devices, LANES), F32)
        for start in range(0, count, LANES):
            size = min(LANES, count - start)
            owner = owner_refs[kind][:, start : start + size]
            row = row_refs[kind][:, start : start + size]
            if size < LANES:
                owner = jnp.concatenate([owner, jnp.full((1, LANES - size), -1, jnp.int32)], axis=1)
                row = jnp.concatenate([row, jnp.zeros((1, LANES - size), jnp.int32)], axis=1)
            hot = jnp.where(device == owner, 1.0, 0.0)
            ranks = jnp.dot(hot.astype(BF16), earlier, preferred_element_type=F32)
            prior = ranks[:, :LANES] + carried
            carried = carried + ranks[:, LANES:]
            position = jnp.sum(hot * prior, axis=0, keepdims=True).astype(jnp.int32) + offsets[kind]
            slot_ref[block : block + 1, :] = jnp.maximum(owner, 0) * stride + 2 * position
            high = (row // LANES).astype(F32)
            low = (row % LANES).astype(F32)
            halves = jnp.concatenate([hot * high, hot * low], axis=0).astype(BF16)
            spread = jnp.where(place == position, 1.0, 0.0).astype(BF16)
            total = total + lax.dot_general(
                halves, spread, (((1,), (1,)), ((), ())), preferred_element_type=F32
            )
            block += 1
    request = (total[:devices] * (2.0 * LANES) + total[devices:] * 2.0).astype(jnp.int32)
    request_ref[...] = request.reshape(devices, 1, width)


def gather_kernel(slots, chunk, request_ref, table_ref, out_ref, staged, wide, packed, sems):
    devices = out_ref.shape[0]
    rows = table_ref.shape[0]
    pieces = rows // chunk

    def copy(piece):
        span = pl.ds(piece * chunk, chunk)
        return pltpu.make_async_copy(table_ref.at[span], staged.at[span], sems.at[piece])

    for piece in range(pieces):
        copy(piece).start()
    step = min(chunk, 256)
    for piece in range(pieces):
        copy(piece).wait()

        def widen(index, _):
            base = pl.multiple_of(piece * chunk + index * step, step)
            values = staged[pl.ds(base, step), :].astype(F32)
            wide[pl.ds(2 * base, step, stride=2), :] = values[:, :LANES]
            wide[pl.ds(2 * base + 1, step, stride=2), :] = values[:, LANES:]
            return 0

        lax.fori_loop(0, chunk // step, widen, 0)

    def serve(device, _):
        for slot in range(slots):
            row = pl.multiple_of(request_ref[device, 0, slot], 2)
            packed[pl.ds(2 * slot, 2), :] = wide[pl.ds(row, 2), :]
        out_ref[device] = packed[: 2 * slots, :].astype(BF16)
        return 0

    lax.fori_loop(0, devices, serve, 0)


def layer(selves, neighbours, share, weights):
    pieces = list(selves)
    fan = len(neighbours)
    for relation in range(R):
        for half in range(2):
            merged = share(relation, 0) * neighbours[0][half]
            for k in range(1, fan):
                merged = merged + share(relation, k) * neighbours[k][half]
            pieces.append(merged)
    inputs = jnp.concatenate([piece.astype(BF16) for piece in pieces], axis=1)
    return jnp.dot(inputs, weights, preferred_element_type=F32)


def model_kernel(
    counts, stride, slot_ref, got_ref, first_ref, second_ref, share1_ref, share2_ref, mask_ref,
    loss_ref, sums_ref, wide, x0, x1, x2, h_low, h_high,
):
    devices, held, _ = got_ref.shape
    seeds, firsts, _ = counts

    def widen(device, _):
        wide[pl.ds(pl.multiple_of(device * stride, 8), held), :] = got_ref[device].astype(F32)
        return 0

    lax.fori_loop(0, devices, widen, 0)
    block = 0
    for target, count in zip((x0, x1, x2), counts):
        whole = count // LANES

        def fetch(index, _, target=target, block=block):
            base = pl.multiple_of(index * 2 * LANES, 2 * LANES)
            for lane in range(LANES):
                slot = pl.multiple_of(slot_ref[block + index, lane], 2)
                target[pl.ds(base + 2 * lane, 2), :] = wide[pl.ds(slot, 2), :]
            return 0

        lax.fori_loop(0, whole, fetch, 0)
        for lane in range(count - whole * LANES):
            slot = pl.multiple_of(slot_ref[block + whole, lane], 2)
            target[pl.ds(2 * (whole * LANES + lane), 2), :] = wide[pl.ds(slot, 2), :]
        block += -(-count // LANES)

    step = LANES

    def hop(index, _):
        base = pl.multiple_of(index * step, step)
        selves = [x1[pl.ds(2 * base + half, step, stride=2), :] for half in range(2)]
        neighbours = [
            [x2[pl.ds(2 * FAN2 * base + 2 * k + half, step, stride=2 * FAN2), :] for half in range(2)]
            for k in range(FAN2)
        ]
        shares = share2_ref[pl.ds(base, step), :]
        hidden = layer(
            selves, neighbours, lambda r, k: shares[:, r * FAN2 + k : r * FAN2 + k + 1], first_ref[...]
        )
        hidden = jnp.maximum(hidden, 0.0).astype(BF16).astype(F32)
        h_low[pl.ds(base, step), :] = hidden[:, :LANES]
        h_high[pl.ds(base, step), :] = hidden[:, LANES:]
        return 0

    lax.fori_loop(0, firsts // step, hop, 0)
    shares = share1_ref[...]
    share = lambda r, k: shares[:, r * FAN1 + k : r * FAN1 + k + 1]
    selves = [x0[pl.ds(half, seeds, stride=2), :] for half in range(2)]
    neighbours = [
        [x1[pl.ds(2 * k + half, seeds, stride=2 * FAN1), :] for half in range(2)] for k in range(FAN1)
    ]
    hidden = jnp.maximum(layer(selves, neighbours, share, first_ref[...]), 0.0).astype(BF16)
    selves = [hidden[:, :LANES], hidden[:, LANES:]]
    neighbours = [
        [h[pl.ds(k, seeds, stride=FAN1), :] for h in (h_low, h_high)] for k in range(FAN1)
    ]
    second = layer(selves, neighbours, share, second_ref[...])
    positives = mask_ref.shape[1]
    width = second.shape[1]
    contract = (((1,), (1,)), ((), ()))
    loss_sum = jnp.zeros((1, 1), F32)
    for number in range(positives // BLOCK):
        span = slice(number * BLOCK, (number + 1) * BLOCK)
        sources = second[span]
        targets = second[positives + number * BLOCK : positives + (number + 1) * BLOCK]
        negatives = second[2 * positives + number * NEG : 2 * positives + (number + 1) * NEG]
        positive = lax.dot_general(
            jnp.ones((8, width), F32), sources * targets, contract, precision=HIGHEST,
            preferred_element_type=F32,
        )[:1]
        negative = lax.dot_general(
            negatives, sources, contract, precision=HIGHEST, preferred_element_type=F32
        )
        top = jnp.maximum(jnp.max(negative, axis=0, keepdims=True), positive)
        spread = jnp.sum(jnp.exp(negative - top), axis=0, keepdims=True) + jnp.exp(positive - top)
        loss = top + jnp.log(spread) - positive
        loss_ref[:, span] = loss
        loss_sum = loss_sum + jnp.sum(
            mask_ref[:, span].astype(F32) * loss, axis=1, keepdims=True
        )
    edge_sum = jnp.sum(mask_ref[...].astype(F32), axis=1, keepdims=True)
    lane = lax.broadcasted_iota(jnp.int32, (devices, 1, LANES), 2)
    sums_ref[...] = jnp.where(
        lane == 0, loss_sum.reshape(1, 1, 1), jnp.where(lane == 1, edge_sum.reshape(1, 1, 1), 0.0)
    )


def mean_shares(relations):
    onehot = (relations[..., None] == jnp.arange(R, dtype=jnp.int32)).astype(F32)
    tallies = jnp.maximum(jnp.sum(onehot, axis=1), 1.0)
    shares = onehot / tallies[:, None, :]
    return jnp.transpose(shares, (0, 2, 1)).reshape(relations.shape[0], -1)


def exchange(array):
    return lax.all_to_all(array, "dom", split_axis=0, concat_axis=0, tiled=True)


def shards(
    features, w_first, w_second, seed_owner, seed_row, hop1_owner, hop1_row, hop1_rel,
    hop2_owner, hop2_row, hop2_rel, edge_mask,
):
    devices = lax.axis_size("dom")
    nodes, width = features.shape
    owners = (seed_owner, hop1_owner, hop2_owner)
    rows = (seed_row, hop1_row, hop2_row)
    counts = tuple(row.shape[0] for row in rows)
    capacities = [(2 * count + devices - 1) // devices for count in counts]
    offsets = [sum(capacities[:kind]) for kind in range(len(counts))]
    slots = sum(capacities)
    held = 2 * slots
    stride = round_up(held, 8)
    blocks = sum(-(-count // LANES) for count in counts)

    requests, places = pl.pallas_call(
        functools.partial(bucket_kernel, offsets, stride, counts),
        out_shape=(
            jax.ShapeDtypeStruct((devices, 1, round_up(slots, LANES)), jnp.int32),
            jax.ShapeDtypeStruct((blocks, LANES), jnp.int32),
        ),
        in_specs=[full()] * 6,
        out_specs=(full(), full()),
        name="bucket",
    )(*[owner.reshape(1, -1) for owner in owners], *[row.reshape(1, -1) for row in rows])

    arrived = exchange(requests)
    chunk = nodes // 16
    located = pl.pallas_call(
        functools.partial(gather_kernel, slots, chunk),
        out_shape=jax.ShapeDtypeStruct((devices, held, LANES), BF16),
        in_specs=[full(pltpu.SMEM), full(pl.ANY)],
        out_specs=full(),
        scratch_shapes=[
            pltpu.VMEM((nodes, width), BF16),
            pltpu.VMEM((2 * nodes, LANES), F32),
            pltpu.VMEM((stride, LANES), F32),
            pltpu.SemaphoreType.DMA((nodes // chunk,)),
        ],
        name="owner_gather",
    )(arrived, features)
    returned = exchange(located)

    share1 = mean_shares(hop1_rel.reshape(counts[0], FAN1))
    share2 = mean_shares(hop2_rel.reshape(counts[1], FAN2))
    positives = edge_mask.shape[0]
    loss, sums = pl.pallas_call(
        functools.partial(model_kernel, counts, stride),
        out_shape=(
            jax.ShapeDtypeStruct((1, positives), F32),
            jax.ShapeDtypeStruct((devices, 1, LANES), F32),
        ),
        in_specs=[full(pltpu.SMEM)] + [full()] * 6,
        out_specs=(full(), full()),
        scratch_shapes=[pltpu.VMEM((devices * stride, LANES), F32)]
        + [pltpu.VMEM((2 * count, LANES), F32) for count in counts]
        + [pltpu.VMEM((counts[1], LANES), F32)] * 2,
        name="model",
    )(places, returned, w_first, w_second, share1, share2, edge_mask.reshape(1, -1))
    totals = jnp.sum(exchange(sums), axis=(0, 1))
    mean_loss = totals[0] / jnp.maximum(totals[1], 1.0)
    return (loss.reshape(positives), mean_loss)


def solution(mesh):
    placed = (
        P("dom", None), P(), P(), P("dom", None), P("dom"), P("dom", None), P("dom"), P("dom"),
        P("dom", None), P("dom"), P("dom"), P("dom"),
    )
    return jax.shard_map(
        shards, mesh=mesh, in_specs=placed, out_specs=(P("dom"), P()), check_vma=False
    )
```

time: 229 us -> 154 us (0.67)
  local copies, waits for them, and re-layouts: 74 us -> 6.34 us
  waiting for transfers between devices: 51 us -> 83.1 us
  Pallas kernels: 0 us -> 29.4 us
  starting transfers between devices: 29.5 us -> 3.56 us
  other arithmetic: 17 us -> 1.76 us
  matrix products: 14.3 us -> 0 us
  blocking collectives: 38.4 us -> 25.8 us
    gather x6 -> x0, local copies, waits for them, and re-layouts: 48.5 us -> none  [the longest x3 33.1 us: fetch_apart(): features[arrived.reshape(-1)].reshape(devices, capacity, features.shape[1])]
    psum x1 -> x0, blocking collectives: 38.4 us -> none  [shards(): lax.psum((jnp.sum(weights * edge_loss), jnp.sum(weights)), 'dom')]
    all_to_all x6 -> x1, waiting for transfers between devices: 51 us -> 83.1 us  [exchange(): return lax.all_to_all(array, 'dom', split_axis=0, concat_axis=0, tiled=True)]
    pallas_call x0 -> x3, Pallas kernels: none -> 29.4 us  [the longest x1 13.1 us: shards(): pl.pallas_call(functools.partial(gather_kernel, slots, chunk), out_shape=...]
    all_to_all x6 -> x1, starting transfers between devices: 29.5 us -> 3.56 us  [exchange(): return lax.all_to_all(array, 'dom', split_axis=0, concat_axis=0, tiled=True)]
    all_to_all x0 -> x2, blocking collectives: none -> 25.8 us  [exchange(): return lax.all_to_all(array, 'dom', split_axis=0, concat_axis=0, tiled=True)]
    dot_general x10 -> x0, matrix products: 14.3 us -> none  [the longest x3 9.68 us: bucket_rows(): lax.dot_general(slot_hot, halves, (((0,), (0,)), ((), ())), preferred_ele...]
    unnamed x52 -> x4, local copies, waits for them, and re-layouts: 7.83 us -> 0.01 us
  transfers between devices with their start and end apart: 6 -> 1, of which waited for: 4 -> 1; matrix products, arithmetic and copies ran while one was open for 33% -> 2% of each run, Pallas kernels for 0% -> 0%
where the time goes in v1:
time: 154 us; the launch traced here: 153 us
  waiting for transfers between devices  83.1 us (54%)
  Pallas kernels  29.4 us (19%)
  blocking collectives  25.8 us (17%)
  local copies, waits for them, and re-layouts  6.34 us (4%)
  starting transfers between devices  3.56 us (2%)
  between operations  3.29 us (2%)
  other arithmetic  1.76 us (1%)
    all_to_all x1, waiting for transfers between devices, exchange(): return lax.all_to_all(array, 'dom', split_axis=0, concat_axis=0, tiled=True)  83.1 us
    all_to_all x2, blocking collectives, exchange(): return lax.all_to_all(array, 'dom', split_axis=0, concat_axis=0, tiled=True)  25.8 us
    pallas_call x1, Pallas kernels, shards(): pl.pallas_call(functools.partial(gather_kernel, slots, chunk), out_shape=...  13.1 us
    pallas_call x1, Pallas kernels, shards(): pl.pallas_call(functools.partial(model_kernel, counts, stride), out_shape...  12.5 us
    reshape x3, local copies, waits for them, and re-layouts, shards(): row.reshape(1, -1)  3.82 us
    pallas_call x1, Pallas kernels, shards(): pl.pallas_call(functools.partial(bucket_kernel, offsets, stride, counts),...  3.8 us
    all_to_all x1, starting transfers between devices, exchange(): return lax.all_to_all(array, 'dom', split_axis=0, concat_axis=0, tiled=True)  3.56 us
  transfers between devices with their start and end apart: 1, of which 1 were waited for; matrix products, arithmetic and copies ran while one was open for 2% of the time, Pallas kernels for 0%

profile of v1, /device:TPU:0, one launch (start us, length us, event | category | flops | bytes accessed | tf_op | source)
XLA Modules:
  0.0 153.2 jit_solution(15196815103018776275)
XLA Ops:
  0.6 1.2 reshape.50.refs_3_
  1.9 1.3 reshape.51.refs_4_
  3.1 1.3 reshape.52.refs_5_
  4.5 3.8 %bucket.1 = (s32[32,1,256]{2,1,0:T(1,128)}, s32[30,128]{1,0:T(8,128)}) custom-call(s32[1,288]{1,0:T(1,128)} %bitcast.16, s32[1,1152]{1,0:T(1,128)} %bitcast.15, s32[1,2304]{1,0:T(1,128)} %bitcast.14, s32[1,288]{1,0:T(1,128)} %reshape.50.refs_3_, s32[1,1152]{1,0:T(1,128)} %reshape.51.refs_4_, s32[1,2304]{1,0:T(1,128)} %reshape.52.refs_5_), custom_call_target="tpu_custom_call" | custom-call | tf_op jit(solution)/shard_map/bucket/pallas_call | solution.py:232
  8.3 14.7 %all_to_all.15.request_ref = s32[32,1,256]{2,1,0:T(1,128)} all-to-all(s32[32,1,256]{2,1,0:T(1,128)} %get-tuple-element.7), channel_id=1, replica_groups=mesh['dom'=32] {'dom'}, dimensions={0} | all-to-all | bytes 65536 | tf_op jit(solution)/shard_map/all_to_all | solution.py:213
  22.9 13.1 %owner_gather.1 = bf16[32,468,128]{2,1,0:T(8,128)(2,1)} custom-call(s32[32,1,256]{2,1,0:T(1,128)} %all_to_all.15.request_ref, bf16[16384,256]{1,0:T(8,128)(2,1)} %table_ref.1), custom_call_target="tpu_custom_call" | custom-call | tf_op jit(solution)/shard_map/owner_gather/pallas_call | solution.py:245
  36.1 3.6 %all-to-all-start.1 = ((bf16[32,468,128]{2,1,0:T(8,128)(2,1)}), bf16[32,468,128]{2,1,0:T(8,128)(2,1)}, u32[]{:S(2)}, u32[]{:S(2)}) async-start(bf16[32,468,128]{2,1,0:T(8,128)(2,1)} %owner_gather.1), calls=%async_computation.1 | async-start | bytes 7733248 | tf_op jit(solution)/shard_map/all_to_all | solution.py:213
  39.7 0.2 eq.58
  39.8 0.1 copy.28
  40.0 0.1 copy.32
  40.2 0.1 copy.29
  40.3 0.1 eq.62
  40.4 0.5 eq.68
  40.9 0.2 copy.33
  41.2 0.2 copy.37
  41.5 0.2 copy.34
  41.8 0.1 eq.72
  41.8 0.7 convert_divide_fusion.1.share1_ref
  42.6 0.9 convert_divide_fusion.share2_ref
  43.5 83.1 %all-to-all-done.1.got_ref = bf16[32,468,128]{2,1,0:T(8,128)(2,1)} async-done(((bf16[32,468,128]{2,1,0:T(8,128)(2,1)}), bf16[32,468,128]{2,1,0:T(8,128)(2,1)}, u32[]{:S(2)}, u32[]{:S(2)}) %all-to-all-start.1) | async-done | bytes 3833888 | tf_op jit(solution)/shard_map/all_to_all | solution.py:213
  126.5 12.5 %model.1 = (f32[1,128]{1,0:T(1,128)}, f32[32,1,128]{2,1,0:T(1,128)}) custom-call(s32[30,128]{1,0:T(8,128)} %get-tuple-element.6.slot_ref, bf16[32,468,128]{2,1,0:T(8,128)(2,1)} %all-to-all-done.1.got_ref, bf16[1280,256]{1,0:T(8,128)(2,1)} %first_ref.1, bf16[1280,256]{1,0:T(8,128)(2,1)} %second_ref.1, f32[288,16]{1,0:T(8,128)} %convert_divide_fusion.1.share1_ref, ...), custom_call_target="tpu_custom_call" | custom-call | tf_op jit(solution)/shard_map/model/pallas_call | solution.py:263
  139.0 11.1 %all_to_all.16 = f32[32,1,128]{2,1,0:T(1,128)S(1)} all-to-all(f32[32,1,128]{2,1,0:T(1,128)} %get-tuple-element.9), channel_id=1, replica_groups=mesh['dom'=32] {'dom'}, dimensions={0} | all-to-all | bytes 32768 | tf_op jit(solution)/shard_map/all_to_all | solution.py:213
  150.1 0.1 reduce_sum.29
  150.2 0.6 fusion
  (18 shorter events, 0.2 us)
Async XLA Ops:
  36.1 3.6 %copy-start.1 = (s32[1152]{0:T(1024)S(1)}, s32[1152]{0:T(1024)}, u32[]{:S(2)}) copy-start(s32[1152]{0:T(1024)} %param.19) | copy-start | bytes 13828
  36.1 4.3 %copy-start = (s32[2304]{0:T(1024)S(1)}, s32[2304]{0:T(1024)}, u32[]{:S(2)}) copy-start(s32[2304]{0:T(1024)} %param.22) | copy-start | bytes 27652
  36.1 90.4 %all-to-all-start.1 = ((bf16[32,468,128]{2,1,0:T(8,128)(2,1)}), bf16[32,468,128]{2,1,0:T(8,128)(2,1)}, u32[]{:S(2)}, u32[]{:S(2)}) async-start(bf16[32,468,128]{2,1,0:T(8,128)(2,1)} %owner_gather.1), calls=%async_computation.1 | async-start | bytes 7733248 | tf_op jit(solution)/shard_map/all_to_all | solution.py:213

commit v2 on v1

--- a/solution.py
+++ b/solution.py
@@ -26,7 +26,7 @@
     return pl.BlockSpec(memory_space=memory_space)
 
 
-def bucket_kernel(offsets, stride, counts, *refs):
+def bucket_kernel(offsets, starts, strides, counts, *refs):
     kinds = len(counts)
     owner_refs, row_refs = refs[:kinds], refs[kinds : 2 * kinds]
     request_ref, slot_ref = refs[2 * kinds :]
@@ -52,7 +52,9 @@
             prior = ranks[:, :LANES] + carried
             carried = carried + ranks[:, LANES:]
             position = jnp.sum(hot * prior, axis=0, keepdims=True).astype(jnp.int32) + offsets[kind]
-            slot_ref[block : block + 1, :] = jnp.maximum(owner, 0) * stride + 2 * position
+            slot_ref[block : block + 1, :] = (
+                jnp.maximum(owner, 0) * strides[kind] + 2 * (position - starts[kind])
+            )
             high = (row // LANES).astype(F32)
             low = (row % LANES).astype(F32)
             halves = jnp.concatenate([hot * high, hot * low], axis=0).astype(BF16)
@@ -65,7 +67,7 @@
     request_ref[...] = request.reshape(devices, 1, width)
 
 
-def gather_kernel(slots, chunk, request_ref, table_ref, out_ref, staged, wide, packed, sems):
+def gather_kernel(first, slots, chunk, request_ref, table_ref, out_ref, staged, wide, packed, sems):
     devices = out_ref.shape[0]
     rows = table_ref.shape[0]
     pieces = rows // chunk
@@ -91,7 +93,7 @@
 
     def serve(device, _):
         for slot in range(slots):
-            row = pl.multiple_of(request_ref[device, 0, slot], 2)
+            row = pl.multiple_of(request_ref[device, 0, first + slot], 2)
             packed[pl.ds(2 * slot, 2), :] = wide[pl.ds(row, 2), :]
         out_ref[device] = packed[: 2 * slots, :].astype(BF16)
         return 0
@@ -112,51 +114,50 @@
     return jnp.dot(inputs, weights, preferred_element_type=F32)
 
 
-def model_kernel(
-    counts, stride, slot_ref, got_ref, first_ref, second_ref, share1_ref, share2_ref, mask_ref,
-    loss_ref, sums_ref, wide, x0, x1, x2, h_low, h_high,
-):
+def widen_rows(got_ref, wide, stride):
     devices, held, _ = got_ref.shape
-    seeds, firsts, _ = counts
 
     def widen(device, _):
         wide[pl.ds(pl.multiple_of(device * stride, 8), held), :] = got_ref[device].astype(F32)
         return 0
 
     lax.fori_loop(0, devices, widen, 0)
-    block = 0
-    for target, count in zip((x0, x1, x2), counts):
-        whole = count // LANES
-
-        def fetch(index, _, target=target, block=block):
-            base = pl.multiple_of(index * 2 * LANES, 2 * LANES)
-            for lane in range(LANES):
-                slot = pl.multiple_of(slot_ref[block + index, lane], 2)
-                target[pl.ds(base + 2 * lane, 2), :] = wide[pl.ds(slot, 2), :]
-            return 0
-
-        lax.fori_loop(0, whole, fetch, 0)
-        for lane in range(count - whole * LANES):
-            slot = pl.multiple_of(slot_ref[block + whole, lane], 2)
-            target[pl.ds(2 * (whole * LANES + lane), 2), :] = wide[pl.ds(slot, 2), :]
-        block += -(-count // LANES)
-
+
+
+def fetch_rows(slot_ref, block, wide, target, count):
+    whole = count // LANES
+
+    def fetch(index, _):
+        base = pl.multiple_of(index * 2 * LANES, 2 * LANES)
+        for lane in range(LANES):
+            slot = pl.multiple_of(slot_ref[block + index, lane], 2)
+            target[pl.ds(base + 2 * lane, 2), :] = wide[pl.ds(slot, 2), :]
+        return 0
+
+    lax.fori_loop(0, whole, fetch, 0)
+    for lane in range(count - whole * LANES):
+        slot = pl.multiple_of(slot_ref[block + whole, lane], 2)
+        target[pl.ds(2 * (whole * LANES + lane), 2), :] = wide[pl.ds(slot, 2), :]
+    return block + -(-count // LANES)
+
+
+def early_kernel(
+    seeds, firsts, stride, slot_ref, got_ref, first_ref, share1_ref, hidden_ref, base_ref,
+    wide, x0, x1,
+):
+    widen_rows(got_ref, wide, stride)
+    block = fetch_rows(slot_ref, 0, wide, x0, seeds)
+    fetch_rows(slot_ref, block, wide, x1, firsts)
     step = LANES
+    width = first_ref.shape[1]
 
     def hop(index, _):
         base = pl.multiple_of(index * step, step)
         selves = [x1[pl.ds(2 * base + half, step, stride=2), :] for half in range(2)]
-        neighbours = [
-            [x2[pl.ds(2 * FAN2 * base + 2 * k + half, step, stride=2 * FAN2), :] for half in range(2)]
-            for k in range(FAN2)
-        ]
-        shares = share2_ref[pl.ds(base, step), :]
-        hidden = layer(
-            selves, neighbours, lambda r, k: shares[:, r * FAN2 + k : r * FAN2 + k + 1], first_ref[...]
+        inputs = jnp.concatenate([piece.astype(BF16) for piece in selves], axis=1)
+        base_ref[pl.ds(base, step), :] = jnp.dot(
+            inputs, first_ref[:width, :], preferred_element_type=F32
         )
-        hidden = jnp.maximum(hidden, 0.0).astype(BF16).astype(F32)
-        h_low[pl.ds(base, step), :] = hidden[:, :LANES]
-        h_high[pl.ds(base, step), :] = hidden[:, LANES:]
         return 0
 
     lax.fori_loop(0, firsts // step, hop, 0)
@@ -166,14 +167,47 @@
     neighbours = [
         [x1[pl.ds(2 * k + half, seeds, stride=2 * FAN1), :] for half in range(2)] for k in range(FAN1)
     ]
-    hidden = jnp.maximum(layer(selves, neighbours, share, first_ref[...]), 0.0).astype(BF16)
+    hidden = layer(selves, neighbours, share, first_ref[...])
+    hidden_ref[...] = jnp.maximum(hidden, 0.0).astype(BF16)
+
+
+def late_kernel(
+    block, counts, stride, slot_ref, got_ref, base_ref, hidden_ref, first_ref, second_ref,
+    share1_ref, share2_ref, mask_ref, loss_ref, sums_ref, wide, x2, h_low, h_high,
+):
+    devices = got_ref.shape[0]
+    seeds, firsts, seconds = counts
+    width = first_ref.shape[1]
+    widen_rows(got_ref, wide, stride)
+    fetch_rows(slot_ref, block, wide, x2, seconds)
+    step = LANES
+
+    def hop(index, _):
+        base = pl.multiple_of(index * step, step)
+        neighbours = [
+            [x2[pl.ds(2 * FAN2 * base + 2 * k + half, step, stride=2 * FAN2), :] for half in range(2)]
+            for k in range(FAN2)
+        ]
+        shares = share2_ref[pl.ds(base, step), :]
+        hidden = base_ref[pl.ds(base, step), :] + layer(
+            [], neighbours, lambda r, k: shares[:, r * FAN2 + k : r * FAN2 + k + 1],
+            first_ref[width:, :],
+        )
+        hidden = jnp.maximum(hidden, 0.0).astype(BF16).astype(F32)
+        h_low[pl.ds(base, step), :] = hidden[:, :LANES]
+        h_high[pl.ds(base, step), :] = hidden[:, LANES:]
+        return 0
+
+    lax.fori_loop(0, firsts // step, hop, 0)
+    shares = share1_ref[...]
+    share = lambda r, k: shares[:, r * FAN1 + k : r * FAN1 + k + 1]
+    hidden = hidden_ref[...]
     selves = [hidden[:, :LANES], hidden[:, LANES:]]
     neighbours = [
         [h[pl.ds(k, seeds, stride=FAN1), :] for h in (h_low, h_high)] for k in range(FAN1)
     ]
     second = layer(selves, neighbours, share, second_ref[...])
     positives = mask_ref.shape[1]
-    width = second.shape[1]
     contract = (((1,), (1,)), ((), ()))
     loss_sum = jnp.zeros((1, 1), F32)
     for number in range(positives // BLOCK):
@@ -225,15 +259,19 @@
     capacities = [(2 * count + devices - 1) // devices for count in counts]
     offsets = [sum(capacities[:kind]) for kind in range(len(counts))]
     slots = sum(capacities)
-    held = 2 * slots
-    stride = round_up(held, 8)
-    blocks = sum(-(-count // LANES) for count in counts)
+    groups = ((0, offsets[2]), (offsets[2], slots))
+    pitches = [round_up(2 * (end - start), 8) for start, end in groups]
+    group_of = (0, 0, 1)
+    blocks = [-(-count // LANES) for count in counts]
 
     requests, places = pl.pallas_call(
-        functools.partial(bucket_kernel, offsets, stride, counts),
+        functools.partial(
+            bucket_kernel, offsets, [groups[g][0] for g in group_of],
+            [pitches[g] for g in group_of], counts,
+        ),
         out_shape=(
             jax.ShapeDtypeStruct((devices, 1, round_up(slots, LANES)), jnp.int32),
-            jax.ShapeDtypeStruct((blocks, LANES), jnp.int32),
+            jax.ShapeDtypeStruct((sum(blocks), LANES), jnp.int32),
         ),
         in_specs=[full()] * 6,
         out_specs=(full(), full()),
@@ -242,37 +280,58 @@
 
     arrived = exchange(requests)
     chunk = nodes // 16
-    located = pl.pallas_call(
-        functools.partial(gather_kernel, slots, chunk),
-        out_shape=jax.ShapeDtypeStruct((devices, held, LANES), BF16),
-        in_specs=[full(pltpu.SMEM), full(pl.ANY)],
-        out_specs=full(),
-        scratch_shapes=[
-            pltpu.VMEM((nodes, width), BF16),
-            pltpu.VMEM((2 * nodes, LANES), F32),
-            pltpu.VMEM((stride, LANES), F32),
-            pltpu.SemaphoreType.DMA((nodes // chunk,)),
-        ],
-        name="owner_gather",
-    )(arrived, features)
-    returned = exchange(located)
+
+    def locate(start, end):
+        held = 2 * (end - start)
+        return pl.pallas_call(
+            functools.partial(gather_kernel, start, end - start, chunk),
+            out_shape=jax.ShapeDtypeStruct((devices, held, LANES), BF16),
+            in_specs=[full(pltpu.SMEM), full(pl.ANY)],
+            out_specs=full(),
+            scratch_shapes=[
+                pltpu.VMEM((nodes, width), BF16),
+                pltpu.VMEM((2 * nodes, LANES), F32),
+                pltpu.VMEM((round_up(held, 8), LANES), F32),
+                pltpu.SemaphoreType.DMA((nodes // chunk,)),
+            ],
+            cost_estimate=pl.CostEstimate(flops=20_000_000, bytes_accessed=nodes * width * 2, transcendentals=0),
+            name="owner_gather",
+        )(arrived, features)
 
     share1 = mean_shares(hop1_rel.reshape(counts[0], FAN1))
     share2 = mean_shares(hop2_rel.reshape(counts[1], FAN2))
+    located = locate(*groups[0])
+    near = exchange(located)
+    located = locate(*groups[1])
+    far = exchange(located)
+    hidden, base = pl.pallas_call(
+        functools.partial(early_kernel, counts[0], counts[1], pitches[0]),
+        out_shape=(
+            jax.ShapeDtypeStruct((counts[0], width), BF16),
+            jax.ShapeDtypeStruct((counts[1], width), F32),
+        ),
+        in_specs=[full(pltpu.SMEM)] + [full()] * 3,
+        out_specs=(full(), full()),
+        scratch_shapes=[pltpu.VMEM((devices * pitches[0], LANES), F32)]
+        + [pltpu.VMEM((2 * count, LANES), F32) for count in counts[:2]],
+        name="early",
+    )(places, near, w_first, share1)
     positives = edge_mask.shape[0]
     loss, sums = pl.pallas_call(
-        functools.partial(model_kernel, counts, stride),
+        functools.partial(late_kernel, blocks[0] + blocks[1], counts, pitches[1]),
         out_shape=(
             jax.ShapeDtypeStruct((1, positives), F32),
             jax.ShapeDtypeStruct((devices, 1, LANES), F32),
         ),
-        in_specs=[full(pltpu.SMEM)] + [full()] * 6,
+        in_specs=[full(pltpu.SMEM)] + [full()] * 8,
         out_specs=(full(), full()),
-        scratch_shapes=[pltpu.VMEM((devices * stride, LANES), F32)]
-        + [pltpu.VMEM((2 * count, LANES), F32) for count in counts]
+        scratch_shapes=[
+            pltpu.VMEM((devices * pitches[1], LANES), F32),
+            pltpu.VMEM((2 * counts[2], LANES), F32),
+        ]
         + [pltpu.VMEM((counts[1], LANES), F32)] * 2,
-        name="model",
-    )(places, returned, w_first, w_second, share1, share2, edge_mask.reshape(1, -1))
+        name="late",
+    )(places, far, base, hidden, w_first, w_second, share1, share2, edge_mask.reshape(1, -1))
     totals = jnp.sum(exchange(sums), axis=(0, 1))
     mean_loss = totals[0] / jnp.maximum(totals[1], 1.0)
     return (loss.reshape(positives), mean_loss)

time: 154 us -> 157 us (1.019)
  waiting for transfers between devices: 83.1 us -> 66.5 us
  Pallas kernels: 29.4 us -> 40.3 us
  local copies, waits for them, and re-layouts: 6.34 us -> 11.7 us
  starting transfers between devices: 3.56 us -> 6.15 us
    all_to_all x1 -> x2, waiting for transfers between devices: 83.1 us -> 66.5 us  [exchange(): return lax.all_to_all(array, 'dom', split_axis=0, concat_axis=0, tiled=True)]
    pallas_call x3 -> x5, Pallas kernels: 29.4 us -> 40.3 us  [the longest x2 19.3 us: locate(): pl.pallas_call(functools.partial(gather_kernel, start, end - start, chunk...]
    all_to_all x1 -> x2, starting transfers between devices: 3.56 us -> 6.15 us  [exchange(): return lax.all_to_all(array, 'dom', split_axis=0, concat_axis=0, tiled=True)]
    unnamed x4 -> x8, local copies, waits for them, and re-layouts: 0.01 us -> 2.58 us
    eq x14, local copies, waits for them, and re-layouts: 1.53 us -> 3.58 us  [mean_shares(): relations[..., None] == jnp.arange(R, dtype=jnp.int32)]
  transfers between devices with their start and end apart: 1 -> 2, of which waited for: 1 -> 2; matrix products, arithmetic and copies ran while one was open for 2% -> 5% of each run, Pallas kernels for 0% -> 11%
where the time goes in v2:
time: 157 us
  waiting for transfers between devices  66.5 us (42%)
  Pallas kernels  40.3 us (26%)
  blocking collectives  26 us (17%)
  local copies, waits for them, and re-layouts  11.7 us (7%)
  starting transfers between devices  6.15 us (4%)
  between operations  3.19 us (2%)
  other arithmetic  2.73 us (2%)
    all_to_all x2, waiting for transfers between devices, exchange(): return lax.all_to_all(array, 'dom', split_axis=0, concat_axis=0, tiled=True)  66.5 us
    all_to_all x2, blocking collectives, exchange(): return lax.all_to_all(array, 'dom', split_axis=0, concat_axis=0, tiled=True)  26 us
    pallas_call x2, Pallas kernels, locate(): pl.pallas_call(functools.partial(gather_kernel, start, end - start, chunk...  19.3 us
    pallas_call x1, Pallas kernels, shards(): pl.pallas_call(functools.partial(late_kernel, blocks[0] + blocks[1], coun...  10.8 us
    pallas_call x1, Pallas kernels, shards(): pl.pallas_call(functools.partial(early_kernel, counts[0], counts[1], pitc...  6.33 us
    all_to_all x2, starting transfers between devices, exchange(): return lax.all_to_all(array, 'dom', split_axis=0, concat_axis=0, tiled=True)  6.15 us
    reshape x3, local copies, waits for them, and re-layouts, shards(): row.reshape(1, -1)  3.87 us
    pallas_call x1, Pallas kernels, shards(): pl.pallas_call(functools.partial(bucket_kernel, offsets, [groups[g][0] fo...  3.81 us
  transfers between devices with their start and end apart: 2, of which 2 were waited for; matrix products, arithmetic and copies ran while one was open for 5% of the time, Pallas kernels for 11%

profile of v2, /device:TPU:0, one launch (start us, length us, event | category | flops | bytes accessed | tf_op | source)
XLA Modules:
  0.0 156.5 jit_solution(16329791755993895142)
XLA Ops:
  0.6 1.3 reshape.50.refs_3_
  1.9 1.3 reshape.51.refs_4_
  3.2 1.3 reshape.52.refs_5_
  4.5 3.8 %bucket.1 = (s32[32,1,256]{2,1,0:T(1,128)}, s32[30,128]{1,0:T(8,128)}) custom-call(s32[1,288]{1,0:T(1,128)} %bitcast.16, s32[1,1152]{1,0:T(1,128)} %bitcast.15, s32[1,2304]{1,0:T(1,128)} %bitcast.14, s32[1,288]{1,0:T(1,128)} %reshape.50.refs_3_, s32[1,1152]{1,0:T(1,128)} %reshape.51.refs_4_, s32[1,2304]{1,0:T(1,128)} %reshape.52.refs_5_), custom_call_target="tpu_custom_call" | custom-call | tf_op jit(solution)/shard_map/bucket/pallas_call | solution.py:267
  8.3 14.7 %all_to_all.20.request_ref = s32[32,1,256]{2,1,0:T(1,128)} all-to-all(s32[32,1,256]{2,1,0:T(1,128)} %get-tuple-element.9), channel_id=1, replica_groups=mesh['dom'=32] {'dom'}, dimensions={0} | all-to-all | bytes 65536 | tf_op jit(solution)/shard_map/all_to_all | solution.py:247
  23.0 8.9 %owner_gather.3 = bf16[32,180,128]{2,1,0:T(8,128)(2,1)} custom-call(s32[32,1,256]{2,1,0:T(1,128)} %all_to_all.20.request_ref, bf16[16384,256]{1,0:T(8,128)(2,1)} %table_ref.3), custom_call_target="tpu_custom_call" | custom-call | flops 20000000 | bytes 8388608 | tf_op jit(solution)/shard_map/owner_gather/pallas_call | solution.py:286
  31.9 2.7 %all-to-all-start.2 = ((bf16[32,180,128]{2,1,0:T(8,128)(2,1)}), bf16[32,180,128]{2,1,0:T(8,128)(2,1)S(1)}, u32[]{:S(2)}, u32[]{:S(2)}) async-start(bf16[32,180,128]{2,1,0:T(8,128)(2,1)} %owner_gather.3), calls=%async_computation.2 | async-start | bytes 3014656 | tf_op jit(solution)/shard_map/all_to_all | solution.py:247
  34.6 10.4 %owner_gather.2 = bf16[32,288,128]{2,1,0:T(8,128)(2,1)} custom-call(s32[32,1,256]{2,1,0:T(1,128)} %all_to_all.20.request_ref, bf16[16384,256]{1,0:T(8,128)(2,1)} %table_ref.3), custom_call_target="tpu_custom_call" | custom-call | flops 20000000 | bytes 8388608 | tf_op jit(solution)/shard_map/owner_gather/pallas_call | solution.py:286
  45.1 25.9 %all-to-all-done.2.got_ref = bf16[32,180,128]{2,1,0:T(8,128)(2,1)S(1)} async-done(((bf16[32,180,128]{2,1,0:T(8,128)(2,1)}), bf16[32,180,128]{2,1,0:T(8,128)(2,1)S(1)}, u32[]{:S(2)}, u32[]{:S(2)}) %all-to-all-start.2) | async-done | bytes 1474592 | tf_op jit(solution)/shard_map/all_to_all | solution.py:247
  71.0 1.1 copy-done.1
  72.1 3.5 %all-to-all-start.1 = ((bf16[32,288,128]{2,1,0:T(8,128)(2,1)}), bf16[32,288,128]{2,1,0:T(8,128)(2,1)S(1)}, u32[]{:S(2)}, u32[]{:S(2)}) async-start(bf16[32,288,128]{2,1,0:T(8,128)(2,1)} %owner_gather.2), calls=%async_computation.1 | async-start | bytes 4718592 | tf_op jit(solution)/shard_map/all_to_all | solution.py:247
  75.9 0.8 copy.32
  76.7 0.8 copy.29
  77.6 0.5 eq.68
  78.7 0.6 eq.70
  79.3 1.0 copy.34
  80.4 1.7 %convert_divide_fusion.1.share1_ref = f32[288,16]{1,0:T(8,128)} fusion(f32[288,16]{1,0:T(8,128)} %copy.32, s32[288,16]{1,0:T(8,128)} %copy.29, s32[16]{0:T(128)S(1)} %eq.62), kind=kLoop, calls=%fused_computation.1 | loop fusion | flops 13824 | bytes 55360 | tf_op jit(solution)/shard_map/div | solution.py:242
  82.1 0.9 convert_divide_fusion.share2_ref
  83.0 6.3 %early.1 = (bf16[288,256]{1,0:T(8,128)(2,1)}, f32[1152,256]{1,0:T(8,128)}) custom-call(s32[30,128]{1,0:T(8,128)} %get-tuple-element.8.slot_ref, bf16[32,180,128]{2,1,0:T(8,128)(2,1)} %copy-done.1, bf16[1280,256]{1,0:T(8,128)(2,1)} %first_ref.3, f32[288,16]{1,0:T(8,128)} %convert_divide_fusion.1.share1_ref), custom_call_target="tpu_custom_call" | custom-call | tf_op jit(solution)/shard_map/early/pallas_call | solution.py:307
  89.3 40.6 %all-to-all-done.1.got_ref = bf16[32,288,128]{2,1,0:T(8,128)(2,1)S(1)} async-done(((bf16[32,288,128]{2,1,0:T(8,128)(2,1)}), bf16[32,288,128]{2,1,0:T(8,128)(2,1)S(1)}, u32[]{:S(2)}, u32[]{:S(2)}) %all-to-all-start.1) | async-done | bytes 2359328 | tf_op jit(solution)/shard_map/all_to_all | solution.py:247
  130.0 1.4 copy-done
  131.4 10.8 %late.1 = (f32[1,128]{1,0:T(1,128)}, f32[32,1,128]{2,1,0:T(1,128)}) custom-call(s32[30,128]{1,0:T(8,128)} %get-tuple-element.8.slot_ref, bf16[32,288,128]{2,1,0:T(8,128)(2,1)} %copy-done, f32[1152,256]{1,0:T(8,128)} %get-tuple-element.10.base_ref, bf16[288,256]{1,0:T(8,128)(2,1)} %get-tuple-element.11.hidden_ref, bf16[1280,256]{1,0:T(8,128)(2,1)} %first_ref.3, ...), custom_call_target="tpu_custom_call" | custom-call | tf_op jit(solution)/shard_map/late/pallas_call | solution.py:320
  142.2 11.3 %all_to_all.21 = f32[32,1,128]{2,1,0:T(1,128)S(1)} all-to-all(f32[32,1,128]{2,1,0:T(1,128)} %get-tuple-element.13), channel_id=1, replica_groups=mesh['dom'=32] {'dom'}, dimensions={0} | all-to-all | bytes 32768 | tf_op jit(solution)/shard_map/all_to_all | solution.py:247
  153.5 0.6 fusion
  (26 shorter events, 1.1 us)
Async XLA Ops:
  31.9 39.1 %all-to-all-start.2 = ((bf16[32,180,128]{2,1,0:T(8,128)(2,1)}), bf16[32,180,128]{2,1,0:T(8,128)(2,1)S(1)}, u32[]{:S(2)}, u32[]{:S(2)}) async-start(bf16[32,180,128]{2,1,0:T(8,128)(2,1)} %owner_gather.3), calls=%async_computation.2 | async-start | bytes 3014656 | tf_op jit(solution)/shard_map/all_to_all | solution.py:247
  45.0 30.5 %copy-start.3 = (s32[1152]{0:T(1024)S(1)}, s32[1152]{0:T(1024)}, u32[]{:S(2)}) copy-start(s32[1152]{0:T(1024)} %param.19) | copy-start | bytes 13828
  45.1 32.5 %copy-start.2 = (s32[2304]{0:T(1024)S(1)}, s32[2304]{0:T(1024)}, u32[]{:S(2)}) copy-start(s32[2304]{0:T(1024)} %param.22) | copy-start | bytes 27652
  71.0 1.1 copy-start.1
  72.1 57.9 %all-to-all-start.1 = ((bf16[32,288,128]{2,1,0:T(8,128)(2,1)}), bf16[32,288,128]{2,1,0:T(8,128)(2,1)S(1)}, u32[]{:S(2)}, u32[]{:S(2)}) async-start(bf16[32,288,128]{2,1,0:T(8,128)(2,1)} %owner_gather.2), calls=%async_computation.1 | async-start | bytes 4718592 | tf_op jit(solution)/shard_map/all_to_all | solution.py:247
  130.0 1.4 copy-start

commit v3 on v1

--- a/solution.py
+++ b/solution.py
@@ -13,6 +13,8 @@
 FAN1 = 4
 FAN2 = 2
 LANES = 128
+PARTS = 4
+HOP_STEP = 384
 F32 = jnp.float32
 BF16 = jnp.bfloat16
 HIGHEST = lax.Precision.HIGHEST
@@ -43,7 +45,7 @@
         for start in range(0, count, LANES):
             size = min(LANES, count - start)
             owner = owner_refs[kind][:, start : start + size]
-            row = row_refs[kind][:, start : start + size]
+            row = row_refs[kind][pl.ds(start, size)].reshape(1, size)
             if size < LANES:
                 owner = jnp.concatenate([owner, jnp.full((1, LANES - size), -1, jnp.int32)], axis=1)
                 row = jnp.concatenate([row, jnp.zeros((1, LANES - size), jnp.int32)], axis=1)
@@ -65,10 +67,14 @@
     request_ref[...] = request.reshape(devices, 1, width)
 
 
-def gather_kernel(slots, chunk, request_ref, table_ref, out_ref, staged, wide, packed, sems):
+def gather_kernel(
+    slots, chunk, group, request_ref, table_ref, out_ref, request, staged, wide, packed, rows_out,
+    request_sem, sems, out_sems,
+):
     devices = out_ref.shape[0]
-    rows = table_ref.shape[0]
-    pieces = rows // chunk
+    pieces = table_ref.shape[0] // chunk
+    asked = pltpu.make_async_copy(request_ref, request, request_sem)
+    asked.start()
 
     def copy(piece):
         span = pl.ds(piece * chunk, chunk)
@@ -88,15 +94,24 @@
             return 0
 
         lax.fori_loop(0, chunk // step, widen, 0)
+    asked.wait()
 
     def serve(device, _):
         for slot in range(slots):
-            row = pl.multiple_of(request_ref[device, 0, slot], 2)
+            row = pl.multiple_of(request[device, 0, slot], 2)
             packed[pl.ds(2 * slot, 2), :] = wide[pl.ds(row, 2), :]
-        out_ref[device] = packed[: 2 * slots, :].astype(BF16)
+        rows_out[device] = packed[: 2 * slots, :].astype(BF16)
         return 0
 
-    lax.fori_loop(0, devices, serve, 0)
+    def leave(part):
+        span = pl.ds(part * group, group)
+        return pltpu.make_async_copy(rows_out.at[span], out_ref.at[span], out_sems.at[part])
+
+    for part in range(devices // group):
+        lax.fori_loop(part * group, (part + 1) * group, serve, 0)
+        leave(part).start()
+    for part in range(devices // group):
+        leave(part).wait()
 
 
 def layer(selves, neighbours, share, weights):
@@ -113,17 +128,36 @@
 
 
 def model_kernel(
-    counts, stride, slot_ref, got_ref, first_ref, second_ref, share1_ref, share2_ref, mask_ref,
-    loss_ref, sums_ref, wide, x0, x1, x2, h_low, h_high,
+    counts, stride, group, slot_hbm, got_hbm, first_hbm, second_hbm, share1_ref, share2_ref, mask_ref,
+    loss_ref, sums_ref, slot_ref, got, first_ref, second_ref, wide, x0, x1, x2, h_low, h_high, sems,
+    got_sems,
 ):
-    devices, held, _ = got_ref.shape
+    devices, held, _ = got_hbm.shape
     seeds, firsts, _ = counts
 
+    def arrive(part):
+        span = pl.ds(part * group, group)
+        return pltpu.make_async_copy(got_hbm.at[span], got.at[span], got_sems.at[part])
+
+    for part in range(devices // group):
+        arrive(part).start()
+    side = [
+        pltpu.make_async_copy(source, target, sems.at[number])
+        for number, (source, target) in enumerate(
+            ((slot_hbm, slot_ref), (first_hbm, first_ref), (second_hbm, second_ref))
+        )
+    ]
+    for copy in side:
+        copy.start()
+
     def widen(device, _):
-        wide[pl.ds(pl.multiple_of(device * stride, 8), held), :] = got_ref[device].astype(F32)
+        wide[pl.ds(pl.multiple_of(device * stride, 8), held), :] = got[device].astype(F32)
         return 0
 
-    lax.fori_loop(0, devices, widen, 0)
+    for part in range(devices // group):
+        arrive(part).wait()
+        lax.fori_loop(part * group, (part + 1) * group, widen, 0)
+    side[0].wait()
     block = 0
     for target, count in zip((x0, x1, x2), counts):
         whole = count // LANES
@@ -141,7 +175,9 @@
             target[pl.ds(2 * (whole * LANES + lane), 2), :] = wide[pl.ds(slot, 2), :]
         block += -(-count // LANES)
 
-    step = LANES
+    step = HOP_STEP
+    side[1].wait()
+    side[2].wait()
 
     def hop(index, _):
         base = pl.multiple_of(index * step, step)
@@ -238,20 +274,25 @@
         in_specs=[full()] * 6,
         out_specs=(full(), full()),
         name="bucket",
-    )(*[owner.reshape(1, -1) for owner in owners], *[row.reshape(1, -1) for row in rows])
+    )(*[owner.reshape(1, -1) for owner in owners], *rows)
 
     arrived = exchange(requests)
     chunk = nodes // 16
+    group = devices // PARTS
     located = pl.pallas_call(
-        functools.partial(gather_kernel, slots, chunk),
+        functools.partial(gather_kernel, slots, chunk, group),
         out_shape=jax.ShapeDtypeStruct((devices, held, LANES), BF16),
-        in_specs=[full(pltpu.SMEM), full(pl.ANY)],
-        out_specs=full(),
+        in_specs=[full(pl.ANY), full(pl.ANY)],
+        out_specs=full(pl.ANY),
         scratch_shapes=[
+            pltpu.SMEM(arrived.shape, jnp.int32),
             pltpu.VMEM((nodes, width), BF16),
             pltpu.VMEM((2 * nodes, LANES), F32),
             pltpu.VMEM((stride, LANES), F32),
+            pltpu.VMEM((devices, held, LANES), BF16),
+            pltpu.SemaphoreType.DMA,
             pltpu.SemaphoreType.DMA((nodes // chunk,)),
+            pltpu.SemaphoreType.DMA((PARTS,)),
         ],
         name="owner_gather",
     )(arrived, features)
@@ -261,16 +302,23 @@
     share2 = mean_shares(hop2_rel.reshape(counts[1], FAN2))
     positives = edge_mask.shape[0]
     loss, sums = pl.pallas_call(
-        functools.partial(model_kernel, counts, stride),
+        functools.partial(model_kernel, counts, stride, group),
         out_shape=(
             jax.ShapeDtypeStruct((1, positives), F32),
             jax.ShapeDtypeStruct((devices, 1, LANES), F32),
         ),
-        in_specs=[full(pltpu.SMEM)] + [full()] * 6,
+        in_specs=[full(pl.ANY)] * 4 + [full()] * 3,
         out_specs=(full(), full()),
-        scratch_shapes=[pltpu.VMEM((devices * stride, LANES), F32)]
+        scratch_shapes=[
+            pltpu.SMEM((blocks, LANES), jnp.int32),
+            pltpu.VMEM((devices, held, LANES), BF16),
+            pltpu.VMEM(w_first.shape, BF16),
+            pltpu.VMEM(w_second.shape, BF16),
+            pltpu.VMEM((devices * stride, LANES), F32),
+        ]
         + [pltpu.VMEM((2 * count, LANES), F32) for count in counts]
-        + [pltpu.VMEM((counts[1], LANES), F32)] * 2,
+        + [pltpu.VMEM((counts[1], LANES), F32)] * 2
+        + [pltpu.SemaphoreType.DMA((3,)), pltpu.SemaphoreType.DMA((PARTS,))],
         name="model",
     )(places, returned, w_first, w_second, share1, share2, edge_mask.reshape(1, -1))
     totals = jnp.sum(exchange(sums), axis=(0, 1))

time: 154 us -> 147 us (0.955)
  local copies, waits for them, and re-layouts: 6.34 us -> 2.52 us
  Pallas kernels: 29.4 us -> 26.2 us
    reshape x3 -> x0, local copies, waits for them, and re-layouts: 3.82 us -> none  [shards(): row.reshape(1, -1)]
    pallas_call x2, Pallas kernels: 25.6 us -> 22.4 us  [the longest x1 11.4 us: shards(): pl.pallas_call(functools.partial(model_kernel, counts, stride, group), ou...]
where the time goes in v3:
time: 147 us; the launch traced here: 146 us
  waiting for transfers between devices  83.1 us (57%)
  Pallas kernels  26.2 us (18%)
  blocking collectives  25.8 us (18%)
  starting transfers between devices  3.56 us (2%)
  between operations  3.3 us (2%)
  local copies, waits for them, and re-layouts  2.52 us (2%)
  other arithmetic  1.76 us (1%)
    all_to_all x1, waiting for transfers between devices, exchange(): return lax.all_to_all(array, 'dom', split_axis=0, concat_axis=0, tiled=True)  83.1 us
    all_to_all x2, blocking collectives, exchange(): return lax.all_to_all(array, 'dom', split_axis=0, concat_axis=0, tiled=True)  25.8 us
    pallas_call x1, Pallas kernels, shards(): pl.pallas_call(functools.partial(model_kernel, counts, stride, group), ou...  11.4 us
    pallas_call x1, Pallas kernels, shards(): pl.pallas_call(functools.partial(gather_kernel, slots, chunk, group), out...  11 us
    pallas_call x1, Pallas kernels, shards(): pl.pallas_call(functools.partial(bucket_kernel, offsets, stride, counts),...  3.81 us
    all_to_all x1, starting transfers between devices, exchange(): return lax.all_to_all(array, 'dom', split_axis=0, concat_axis=0, tiled=True)  3.56 us
  transfers between devices with their start and end apart: 1, of which 1 were waited for; matrix products, arithmetic and copies ran while one was open for 2% of the time, Pallas kernels for 0%

profile of v3, /device:TPU:0, one launch (start us, length us, event | category | flops | bytes accessed | tf_op | source)
XLA Modules:
  0.0 146.2 jit_solution(13394335848263280912)
XLA Ops:
  0.6 3.8 %bucket.1 = (s32[32,1,256]{2,1,0:T(1,128)}, s32[30,128]{1,0:T(8,128)}) custom-call(s32[1,288]{1,0:T(1,128)} %bitcast.16, s32[1,1152]{1,0:T(1,128)} %bitcast.15, s32[1,2304]{1,0:T(1,128)} %bitcast.14, s32[288]{0:T(512)} %refs_3_.1, s32[1152]{0:T(1024)} %refs_4_.1, s32[2304]{0:T(1024)} %refs_5_.1), custom_call_target="tpu_custom_call" | custom-call | tf_op jit(solution)/shard_map/bucket/pallas_call | solution.py:268
  4.4 14.7 %all_to_all.15.request_ref = s32[32,1,256]{2,1,0:T(1,128)} all-to-all(s32[32,1,256]{2,1,0:T(1,128)} %get-tuple-element.7), channel_id=1, replica_groups=mesh['dom'=32] {'dom'}, dimensions={0} | all-to-all | bytes 65536 | tf_op jit(solution)/shard_map/all_to_all | solution.py:249
  19.1 11.0 %owner_gather.1 = bf16[32,468,128]{2,1,0:T(8,128)(2,1)} custom-call(s32[32,1,256]{2,1,0:T(1,128)} %all_to_all.15.request_ref, bf16[16384,256]{1,0:T(8,128)(2,1)} %table_ref.1), custom_call_target="tpu_custom_call" | custom-call | tf_op jit(solution)/shard_map/owner_gather/pallas_call | solution.py:282
  30.2 0.0 copy-start.1
  30.2 0.0 copy-start
  30.2 3.6 %all-to-all-start.1 = ((bf16[32,468,128]{2,1,0:T(8,128)(2,1)}), bf16[32,468,128]{2,1,0:T(8,128)(2,1)}, u32[]{:S(2)}, u32[]{:S(2)}) async-start(bf16[32,468,128]{2,1,0:T(8,128)(2,1)} %owner_gather.1), calls=%async_computation.1 | async-start | bytes 7733248 | tf_op jit(solution)/shard_map/all_to_all | solution.py:249
  33.8 0.0 copy-done.1
  33.8 0.2 eq.58
  33.9 0.1 copy.28
  34.1 0.1 copy.32
  34.3 0.1 copy.29
  34.4 0.1 eq.62
  34.5 0.5 eq.68
  35.0 0.2 copy.33
  35.3 0.2 copy.37
  35.6 0.2 copy.34
  35.9 0.1 eq.72
  35.9 0.7 convert_divide_fusion.1.share1_ref
  36.7 0.9 convert_divide_fusion.share2_ref
  37.6 83.1 %all-to-all-done.1.got_hbm = bf16[32,468,128]{2,1,0:T(8,128)(2,1)} async-done(((bf16[32,468,128]{2,1,0:T(8,128)(2,1)}), bf16[32,468,128]{2,1,0:T(8,128)(2,1)}, u32[]{:S(2)}, u32[]{:S(2)}) %all-to-all-start.1) | async-done | bytes 3833888 | tf_op jit(solution)/shard_map/all_to_all | solution.py:249
  120.6 11.4 %model.1 = (f32[1,128]{1,0:T(1,128)}, f32[32,1,128]{2,1,0:T(1,128)}) custom-call(s32[30,128]{1,0:T(8,128)} %get-tuple-element.6.slot_hbm, bf16[32,468,128]{2,1,0:T(8,128)(2,1)} %all-to-all-done.1.got_hbm, bf16[1280,256]{1,0:T(8,128)(2,1)} %first_hbm.1, bf16[1280,256]{1,0:T(8,128)(2,1)} %second_hbm.1, f32[288,16]{1,0:T(8,128)} %convert_divide_fusion.1.share1_ref, ...), custom_call_target="tpu_custom_call" | custom-call | tf_op jit(solution)/shard_map/model/pallas_call | solution.py:304
  132.0 11.1 %all_to_all.16 = f32[32,1,128]{2,1,0:T(1,128)S(1)} all-to-all(f32[32,1,128]{2,1,0:T(1,128)} %get-tuple-element.9), channel_id=1, replica_groups=mesh['dom'=32] {'dom'}, dimensions={0} | all-to-all | bytes 32768 | tf_op jit(solution)/shard_map/all_to_all | solution.py:249
  143.1 0.1 reduce_sum.29
  143.2 0.6 fusion
  (15 shorter events, 0.2 us)
Async XLA Ops:
  30.2 3.6 %copy-start.1 = (s32[1152]{0:T(1024)S(1)}, s32[1152]{0:T(1024)}, u32[]{:S(2)}) copy-start(s32[1152]{0:T(1024)} %param.19) | copy-start | bytes 13828
  30.2 4.3 %copy-start = (s32[2304]{0:T(1024)S(1)}, s32[2304]{0:T(1024)}, u32[]{:S(2)}) copy-start(s32[2304]{0:T(1024)} %param.22) | copy-start | bytes 27652
  30.2 90.4 %all-to-all-start.1 = ((bf16[32,468,128]{2,1,0:T(8,128)(2,1)}), bf16[32,468,128]{2,1,0:T(8,128)(2,1)}, u32[]{:S(2)}, u32[]{:S(2)}) async-start(bf16[32,468,128]{2,1,0:T(8,128)(2,1)} %owner_gather.1), calls=%async_computation.1 | async-start | bytes 7733248 | tf_op jit(solution)/shard_map/all_to_all | solution.py:249

commit v4 on v3

--- a/solution.py
+++ b/solution.py
@@ -31,17 +31,15 @@
 def bucket_kernel(offsets, stride, counts, *refs):
     kinds = len(counts)
     owner_refs, row_refs = refs[:kinds], refs[kinds : 2 * kinds]
-    request_ref, slot_ref = refs[2 * kinds :]
+    request_ref, slot_ref, hots, ranks, halves, spread = refs[2 * kinds :]
     devices, _, width = request_ref.shape
     device = lax.broadcasted_iota(jnp.int32, (devices, LANES), 0)
     before = lax.broadcasted_iota(jnp.int32, (LANES, 2 * LANES), 0)
     lane = lax.broadcasted_iota(jnp.int32, (LANES, 2 * LANES), 1)
     earlier = jnp.where(before < lane, 1.0, 0.0).astype(BF16)
     place = lax.broadcasted_iota(jnp.int32, (width, LANES), 0)
-    total = jnp.zeros((2 * devices, width), F32)
-    block = 0
+    entries = []
     for kind, count in enumerate(counts):
-        carried = jnp.zeros((devices, LANES), F32)
         for start in range(0, count, LANES):
             size = min(LANES, count - start)
             owner = owner_refs[kind][:, start : start + size]
@@ -50,19 +48,28 @@
                 owner = jnp.concatenate([owner, jnp.full((1, LANES - size), -1, jnp.int32)], axis=1)
                 row = jnp.concatenate([row, jnp.zeros((1, LANES - size), jnp.int32)], axis=1)
             hot = jnp.where(device == owner, 1.0, 0.0)
-            ranks = jnp.dot(hot.astype(BF16), earlier, preferred_element_type=F32)
-            prior = ranks[:, :LANES] + carried
-            carried = carried + ranks[:, LANES:]
-            position = jnp.sum(hot * prior, axis=0, keepdims=True).astype(jnp.int32) + offsets[kind]
-            slot_ref[block : block + 1, :] = jnp.maximum(owner, 0) * stride + 2 * position
-            high = (row // LANES).astype(F32)
-            low = (row % LANES).astype(F32)
-            halves = jnp.concatenate([hot * high, hot * low], axis=0).astype(BF16)
-            spread = jnp.where(place == position, 1.0, 0.0).astype(BF16)
-            total = total + lax.dot_general(
-                halves, spread, (((1,), (1,)), ((), ())), preferred_element_type=F32
-            )
-            block += 1
+            block = len(entries)
+            hots[block * devices : (block + 1) * devices, :] = hot.astype(BF16)
+            span = slice(block * LANES, (block + 1) * LANES)
+            halves[:devices, span] = (hot * (row // LANES).astype(F32)).astype(BF16)
+            halves[devices:, span] = (hot * (row % LANES).astype(F32)).astype(BF16)
+            entries.append((kind, owner, hot))
+    ranks[...] = jnp.dot(hots[...], earlier, preferred_element_type=F32)
+    carried, current = None, None
+    for block, (kind, owner, hot) in enumerate(entries):
+        if kind != current:
+            carried, current = jnp.zeros((devices, LANES), F32), kind
+        span = slice(block * devices, (block + 1) * devices)
+        prior = ranks[span, :LANES] + carried
+        carried = carried + ranks[span, LANES:]
+        position = jnp.sum(hot * prior, axis=0, keepdims=True).astype(jnp.int32) + offsets[kind]
+        slot_ref[block : block + 1, :] = jnp.maximum(owner, 0) * stride + 2 * position
+        spread[:, block * LANES : (block + 1) * LANES] = jnp.where(
+            place == position, 1.0, 0.0
+        ).astype(BF16)
+    total = lax.dot_general(
+        halves[...], spread[...], (((1,), (1,)), ((), ())), preferred_element_type=F32
+    )
     request = (total[:devices] * (2.0 * LANES) + total[devices:] * 2.0).astype(jnp.int32)
     request_ref[...] = request.reshape(devices, 1, width)
 
@@ -108,7 +115,8 @@
         return pltpu.make_async_copy(rows_out.at[span], out_ref.at[span], out_sems.at[part])
 
     for part in range(devices // group):
-        lax.fori_loop(part * group, (part + 1) * group, serve, 0)
+        for device in range(part * group, (part + 1) * group):
+            serve(device, 0)
         leave(part).start()
     for part in range(devices // group):
         leave(part).wait()
@@ -128,8 +136,8 @@
 
 
 def model_kernel(
-    counts, stride, group, slot_hbm, got_hbm, first_hbm, second_hbm, share1_ref, share2_ref, mask_ref,
-    loss_ref, sums_ref, slot_ref, got, first_ref, second_ref, wide, x0, x1, x2, h_low, h_high, sems,
+    counts, stride, group, slot_hbm, got_hbm, first_hbm, second_hbm, share1_hbm, share2_hbm, mask_hbm,
+    loss_ref, sums_ref, slot_ref, got, first_ref, second_ref, share1_ref, share2_ref, mask_ref, wide, x0, x1, x2, h_low, h_high, sems,
     got_sems,
 ):
     devices, held, _ = got_hbm.shape
@@ -144,7 +152,10 @@
     side = [
         pltpu.make_async_copy(source, target, sems.at[number])
         for number, (source, target) in enumerate(
-            ((slot_hbm, slot_ref), (first_hbm, first_ref), (second_hbm, second_ref))
+            (
+                (slot_hbm, slot_ref), (first_hbm, first_ref), (share2_hbm, share2_ref),
+                (share1_hbm, share1_ref), (second_hbm, second_ref), (mask_hbm, mask_ref),
+            )
         )
     ]
     for copy in side:
@@ -162,22 +173,17 @@
     for target, count in zip((x0, x1, x2), counts):
         whole = count // LANES
 
-        def fetch(index, _, target=target, block=block):
-            base = pl.multiple_of(index * 2 * LANES, 2 * LANES)
-            for lane in range(LANES):
-                slot = pl.multiple_of(slot_ref[block + index, lane], 2)
-                target[pl.ds(base + 2 * lane, 2), :] = wide[pl.ds(slot, 2), :]
-            return 0
-
-        lax.fori_loop(0, whole, fetch, 0)
-        for lane in range(count - whole * LANES):
-            slot = pl.multiple_of(slot_ref[block + whole, lane], 2)
-            target[pl.ds(2 * (whole * LANES + lane), 2), :] = wide[pl.ds(slot, 2), :]
+        for item in range(count):
+            slot = pl.multiple_of(slot_ref[block + item // LANES, item % LANES], 2)
+            target[pl.ds(2 * item, 2), :] = wide[pl.ds(slot, 2), :]
         block += -(-count // LANES)
 
     step = HOP_STEP
     side[1].wait()
     side[2].wait()
+    side[3].wait()
+    side[4].wait()
+    side[5].wait()
 
     def hop(index, _):
         base = pl.multiple_of(index * step, step)
@@ -268,11 +274,17 @@
     requests, places = pl.pallas_call(
         functools.partial(bucket_kernel, offsets, stride, counts),
         out_shape=(
-            jax.ShapeDtypeStruct((devices, 1, round_up(slots, LANES)), jnp.int32),
+            pltpu.VMEM((devices, 1, round_up(slots, LANES)), jnp.int32),
             jax.ShapeDtypeStruct((blocks, LANES), jnp.int32),
         ),
         in_specs=[full()] * 6,
         out_specs=(full(), full()),
+        scratch_shapes=[
+            pltpu.VMEM((blocks * devices, LANES), BF16),
+            pltpu.VMEM((blocks * devices, 2 * LANES), F32),
+            pltpu.VMEM((2 * devices, blocks * LANES), BF16),
+            pltpu.VMEM((round_up(slots, LANES), blocks * LANES), BF16),
+        ],
         name="bucket",
     )(*[owner.reshape(1, -1) for owner in owners], *rows)
 
@@ -305,20 +317,23 @@
         functools.partial(model_kernel, counts, stride, group),
         out_shape=(
             jax.ShapeDtypeStruct((1, positives), F32),
-            jax.ShapeDtypeStruct((devices, 1, LANES), F32),
+            pltpu.VMEM((devices, 1, LANES), F32),
         ),
-        in_specs=[full(pl.ANY)] * 4 + [full()] * 3,
+        in_specs=[full(pl.ANY)] * 7,
         out_specs=(full(), full()),
         scratch_shapes=[
             pltpu.SMEM((blocks, LANES), jnp.int32),
             pltpu.VMEM((devices, held, LANES), BF16),
             pltpu.VMEM(w_first.shape, BF16),
             pltpu.VMEM(w_second.shape, BF16),
+            pltpu.VMEM(share1.shape, F32),
+            pltpu.VMEM(share2.shape, F32),
+            pltpu.VMEM((1, positives), jnp.int32),
             pltpu.VMEM((devices * stride, LANES), F32),
         ]
         + [pltpu.VMEM((2 * count, LANES), F32) for count in counts]
         + [pltpu.VMEM((counts[1], LANES), F32)] * 2
-        + [pltpu.SemaphoreType.DMA((3,)), pltpu.SemaphoreType.DMA((PARTS,))],
+        + [pltpu.SemaphoreType.DMA((6,)), pltpu.SemaphoreType.DMA((PARTS,))],
         name="model",
     )(places, returned, w_first, w_second, share1, share2, edge_mask.reshape(1, -1))
     totals = jnp.sum(exchange(sums), axis=(0, 1))

time: 147 us -> 141 us (0.959)
  Pallas kernels: 26.2 us -> 21.2 us
    pallas_call x1, Pallas kernels: 11.4 us -> 9.47 us  [shards(): pl.pallas_call(functools.partial(model_kernel, counts, stride, group), ou...]
    pallas_call x1, Pallas kernels: 3.81 us -> 2.17 us  [shards(): pl.pallas_call(functools.partial(bucket_kernel, offsets, stride, counts),...]
    pallas_call x1, Pallas kernels: 11 us -> 9.52 us  [shards(): pl.pallas_call(functools.partial(gather_kernel, slots, chunk, group), out...]
  transfers between devices with their start and end apart: 1 -> 1, of which waited for: 1 -> 1; matrix products, arithmetic and copies ran while one was open for 2% -> 3% of each run, Pallas kernels for 0% -> 0%
where the time goes in v4:
time: 141 us
  waiting for transfers between devices  83 us (59%)
  blocking collectives  25.3 us (18%)
  Pallas kernels  21.2 us (15%)
  starting transfers between devices  3.74 us (3%)
  between operations  3.31 us (2%)
  local copies, waits for them, and re-layouts  2.52 us (2%)
  other arithmetic  1.76 us (1%)
    all_to_all x1, waiting for transfers between devices, exchange(): return lax.all_to_all(array, 'dom', split_axis=0, concat_axis=0, tiled=True)  83 us
    all_to_all x2, blocking collectives, exchange(): return lax.all_to_all(array, 'dom', split_axis=0, concat_axis=0, tiled=True)  25.3 us
    pallas_call x1, Pallas kernels, shards(): pl.pallas_call(functools.partial(gather_kernel, slots, chunk, group), out...  9.52 us
    pallas_call x1, Pallas kernels, shards(): pl.pallas_call(functools.partial(model_kernel, counts, stride, group), ou...  9.47 us
    all_to_all x1, starting transfers between devices, exchange(): return lax.all_to_all(array, 'dom', split_axis=0, concat_axis=0, tiled=True)  3.74 us
  transfers between devices with their start and end apart: 1, of which 1 were waited for; matrix products, arithmetic and copies ran while one was open for 3% of the time, Pallas kernels for 0%

profile of v4, /device:TPU:0, one launch (start us, length us, event | category | flops | bytes accessed | tf_op | source)
XLA Modules:
  0.0 140.8 jit_solution(13566052064440872583)
XLA Ops:
  0.6 2.2 %bucket.1 = (s32[32,1,256]{2,1,0:T(1,128)S(1)}, s32[30,128]{1,0:T(8,128)}) custom-call(s32[1,288]{1,0:T(1,128)} %bitcast.16, s32[1,1152]{1,0:T(1,128)} %bitcast.15, s32[1,2304]{1,0:T(1,128)} %bitcast.14, s32[288]{0:T(512)} %refs_3_.1, s32[1152]{0:T(1024)} %refs_4_.1, s32[2304]{0:T(1024)} %refs_5_.1), custom_call_target="tpu_custom_call" | custom-call | tf_op jit(solution)/shard_map/bucket/pallas_call | solution.py:274
  2.8 14.5 %all_to_all.15.request_ref = s32[32,1,256]{2,1,0:T(1,128)} all-to-all(s32[32,1,256]{2,1,0:T(1,128)S(1)} %get-tuple-element.7), channel_id=1, replica_groups=mesh['dom'=32] {'dom'}, dimensions={0} | all-to-all | bytes 65536 | tf_op jit(solution)/shard_map/all_to_all | solution.py:255
  17.3 9.5 %owner_gather.1 = bf16[32,468,128]{2,1,0:T(8,128)(2,1)} custom-call(s32[32,1,256]{2,1,0:T(1,128)} %all_to_all.15.request_ref, bf16[16384,256]{1,0:T(8,128)(2,1)} %table_ref.1), custom_call_target="tpu_custom_call" | custom-call | tf_op jit(solution)/shard_map/owner_gather/pallas_call | solution.py:294
  26.8 0.0 copy-start.1
  26.9 0.0 copy-start
  26.9 3.7 %all-to-all-start.1 = ((bf16[32,468,128]{2,1,0:T(8,128)(2,1)}), bf16[32,468,128]{2,1,0:T(8,128)(2,1)}, u32[]{:S(2)}, u32[]{:S(2)}) async-start(bf16[32,468,128]{2,1,0:T(8,128)(2,1)} %owner_gather.1), calls=%async_computation.1 | async-start | bytes 7733248 | tf_op jit(solution)/shard_map/all_to_all | solution.py:255
  30.6 0.0 copy-done.1
  30.6 0.2 eq.58
  30.8 0.1 copy.28
  31.0 0.1 copy.32
  31.1 0.1 copy.29
  31.2 0.1 eq.62
  31.3 0.5 eq.68
  31.8 0.2 copy.33
  32.2 0.2 copy.37
  32.5 0.2 copy.34
  32.7 0.1 eq.72
  32.8 0.7 convert_divide_fusion.1.share1_hbm
  33.5 0.9 convert_divide_fusion.share2_hbm
  34.4 83.0 %all-to-all-done.1.got_hbm = bf16[32,468,128]{2,1,0:T(8,128)(2,1)} async-done(((bf16[32,468,128]{2,1,0:T(8,128)(2,1)}), bf16[32,468,128]{2,1,0:T(8,128)(2,1)}, u32[]{:S(2)}, u32[]{:S(2)}) %all-to-all-start.1) | async-done | bytes 3833888 | tf_op jit(solution)/shard_map/all_to_all | solution.py:255
  117.4 9.5 %model.1 = (f32[1,128]{1,0:T(1,128)}, f32[32,1,128]{2,1,0:T(1,128)S(1)}) custom-call(s32[30,128]{1,0:T(8,128)} %get-tuple-element.6.slot_hbm, bf16[32,468,128]{2,1,0:T(8,128)(2,1)} %all-to-all-done.1.got_hbm, bf16[1280,256]{1,0:T(8,128)(2,1)} %first_hbm.1, bf16[1280,256]{1,0:T(8,128)(2,1)} %second_hbm.1, f32[288,16]{1,0:T(8,128)} %convert_divide_fusion.1.share1_hbm, ...), custom_call_target="tpu_custom_call" | custom-call | tf_op jit(solution)/shard_map/model/pallas_call | solution.py:316
  126.9 10.8 %all_to_all.16 = f32[32,1,128]{2,1,0:T(1,128)S(1)} all-to-all(f32[32,1,128]{2,1,0:T(1,128)S(1)} %get-tuple-element.9), channel_id=1, replica_groups=mesh['dom'=32] {'dom'}, dimensions={0} | all-to-all | bytes 32768 | tf_op jit(solution)/shard_map/all_to_all | solution.py:255
  137.7 0.1 reduce_sum.29
  137.7 0.6 fusion
  (15 shorter events, 0.2 us)
Async XLA Ops:
  26.8 3.8 %copy-start.1 = (s32[1152]{0:T(1024)S(1)}, s32[1152]{0:T(1024)}, u32[]{:S(2)}) copy-start(s32[1152]{0:T(1024)} %param.19) | copy-start | bytes 13828
  26.9 4.5 %copy-start = (s32[2304]{0:T(1024)S(1)}, s32[2304]{0:T(1024)}, u32[]{:S(2)}) copy-start(s32[2304]{0:T(1024)} %param.22) | copy-start | bytes 27652
  26.9 90.5 %all-to-all-start.1 = ((bf16[32,468,128]{2,1,0:T(8,128)(2,1)}), bf16[32,468,128]{2,1,0:T(8,128)(2,1)}, u32[]{:S(2)}, u32[]{:S(2)}) async-start(bf16[32,468,128]{2,1,0:T(8,128)(2,1)} %owner_gather.1), calls=%async_computation.1 | async-start | bytes 7733248 | tf_op jit(solution)/shard_map/all_to_all | solution.py:255

commit v5 on v4

--- a/solution.py
+++ b/solution.py
@@ -14,7 +14,7 @@
 FAN2 = 2
 LANES = 128
 PARTS = 4
-HOP_STEP = 384
+HOP_STEP = 128
 F32 = jnp.float32
 BF16 = jnp.bfloat16
 HIGHEST = lax.Precision.HIGHEST
@@ -136,19 +136,19 @@
 
 
 def model_kernel(
-    counts, stride, group, slot_hbm, got_hbm, first_hbm, second_hbm, share1_hbm, share2_hbm, mask_hbm,
+    counts, stride, split, slot_hbm, got_hbm, first_hbm, second_hbm, share1_hbm, share2_hbm, mask_hbm,
     loss_ref, sums_ref, slot_ref, got, first_ref, second_ref, share1_ref, share2_ref, mask_ref, wide, x0, x1, x2, h_low, h_high, sems,
     got_sems,
 ):
     devices, held, _ = got_hbm.shape
     seeds, firsts, _ = counts
 
-    def arrive(part):
-        span = pl.ds(part * group, group)
-        return pltpu.make_async_copy(got_hbm.at[span], got.at[span], got_sems.at[part])
-
-    for part in range(devices // group):
-        arrive(part).start()
+    bounds = ((0, split), (split, held))
+
+    def arrive(half):
+        span = pl.ds(bounds[half][0], bounds[half][1] - bounds[half][0])
+        return pltpu.make_async_copy(got_hbm.at[:, span], got.at[:, span], got_sems.at[half])
+
     side = [
         pltpu.make_async_copy(source, target, sems.at[number])
         for number, (source, target) in enumerate(
@@ -158,50 +158,59 @@
             )
         )
     ]
-    for copy in side:
+    side[0].start()
+    for half in range(2):
+        arrive(half).start()
+    for copy in side[1:]:
         copy.start()
 
-    def widen(device, _):
-        wide[pl.ds(pl.multiple_of(device * stride, 8), held), :] = got[device].astype(F32)
-        return 0
-
-    for part in range(devices // group):
-        arrive(part).wait()
-        lax.fori_loop(part * group, (part + 1) * group, widen, 0)
+    def take(half):
+        arrive(half).wait()
+        start, end = bounds[half]
+
+        def widen(device, _):
+            base = pl.multiple_of(device * stride, 8) + start
+            wide[pl.ds(pl.multiple_of(base, 8), end - start), :] = got[
+                device, start:end, :
+            ].astype(F32)
+            return 0
+
+        lax.fori_loop(0, devices, widen, 0)
+
     side[0].wait()
-    block = 0
-    for target, count in zip((x0, x1, x2), counts):
-        whole = count // LANES
-
-        for item in range(count):
+    take(0)
+    firsts_block = -(-seeds // LANES)
+    seconds_block = firsts_block + -(-firsts // LANES)
+
+    def fetch(target, block, start, end):
+        for item in range(start, end):
             slot = pl.multiple_of(slot_ref[block + item // LANES, item % LANES], 2)
             target[pl.ds(2 * item, 2), :] = wide[pl.ds(slot, 2), :]
-        block += -(-count // LANES)
 
     step = HOP_STEP
-    side[1].wait()
-    side[2].wait()
-    side[3].wait()
-    side[4].wait()
-    side[5].wait()
-
-    def hop(index, _):
-        base = pl.multiple_of(index * step, step)
+    fetch(x0, 0, 0, seeds)
+    fetch(x1, firsts_block, 0, firsts)
+    take(1)
+    for number in range(1, len(side)):
+        side[number].wait()
+
+    for base in range(0, firsts, step):
+        fetch(x2, seconds_block, FAN2 * base, FAN2 * (base + step))
         selves = [x1[pl.ds(2 * base + half, step, stride=2), :] for half in range(2)]
         neighbours = [
             [x2[pl.ds(2 * FAN2 * base + 2 * k + half, step, stride=2 * FAN2), :] for half in range(2)]
             for k in range(FAN2)
         ]
-        shares = share2_ref[pl.ds(base, step), :]
+        shares2 = share2_ref[base : base + step, :]
         hidden = layer(
-            selves, neighbours, lambda r, k: shares[:, r * FAN2 + k : r * FAN2 + k + 1], first_ref[...]
+            selves, neighbours,
+            lambda r, k, shares2=shares2: shares2[:, r * FAN2 + k : r * FAN2 + k + 1],
+            first_ref[...],
         )
         hidden = jnp.maximum(hidden, 0.0).astype(BF16).astype(F32)
-        h_low[pl.ds(base, step), :] = hidden[:, :LANES]
-        h_high[pl.ds(base, step), :] = hidden[:, LANES:]
-        return 0
-
-    lax.fori_loop(0, firsts // step, hop, 0)
+        h_low[base : base + step, :] = hidden[:, :LANES]
+        h_high[base : base + step, :] = hidden[:, LANES:]
+
     shares = share1_ref[...]
     share = lambda r, k: shares[:, r * FAN1 + k : r * FAN1 + k + 1]
     selves = [x0[pl.ds(half, seeds, stride=2), :] for half in range(2)]
@@ -244,6 +253,11 @@
     )
 
 
+def mean_kernel(sums_ref, mean_ref):
+    totals = jnp.sum(sums_ref[...], axis=0)
+    mean_ref[...] = totals[:, :1] / jnp.maximum(totals[:, 1:2], 1.0)
+
+
 def mean_shares(relations):
     onehot = (relations[..., None] == jnp.arange(R, dtype=jnp.int32)).astype(F32)
     tallies = jnp.maximum(jnp.sum(onehot, axis=1), 1.0)
@@ -275,7 +289,7 @@
         functools.partial(bucket_kernel, offsets, stride, counts),
         out_shape=(
             pltpu.VMEM((devices, 1, round_up(slots, LANES)), jnp.int32),
-            jax.ShapeDtypeStruct((blocks, LANES), jnp.int32),
+            pltpu.VMEM((blocks, LANES), jnp.int32),
         ),
         in_specs=[full()] * 6,
         out_specs=(full(), full()),
@@ -314,9 +328,9 @@
     share2 = mean_shares(hop2_rel.reshape(counts[1], FAN2))
     positives = edge_mask.shape[0]
     loss, sums = pl.pallas_call(
-        functools.partial(model_kernel, counts, stride, group),
+        functools.partial(model_kernel, counts, stride, round_up(2 * offsets[2], 8)),
         out_shape=(
-            jax.ShapeDtypeStruct((1, positives), F32),
+            pltpu.VMEM((1, positives), F32),
             pltpu.VMEM((devices, 1, LANES), F32),
         ),
         in_specs=[full(pl.ANY)] * 7,
@@ -333,12 +347,18 @@
         ]
         + [pltpu.VMEM((2 * count, LANES), F32) for count in counts]
         + [pltpu.VMEM((counts[1], LANES), F32)] * 2
-        + [pltpu.SemaphoreType.DMA((6,)), pltpu.SemaphoreType.DMA((PARTS,))],
+        + [pltpu.SemaphoreType.DMA((6,)), pltpu.SemaphoreType.DMA((2,))],
         name="model",
     )(places, returned, w_first, w_second, share1, share2, edge_mask.reshape(1, -1))
-    totals = jnp.sum(exchange(sums), axis=(0, 1))
-    mean_loss = totals[0] / jnp.maximum(totals[1], 1.0)
-    return (loss.reshape(positives), mean_loss)
+    mean_loss = pl.pallas_call(
+        mean_kernel,
+        out_shape=jax.ShapeDtypeStruct((1, 1), F32),
+        in_specs=[full()],
+        out_specs=full(),
+        compiler_params=pltpu.CompilerParams(vmem_limit_bytes=2**20),
+        name="mean",
+    )(exchange(sums))
+    return (loss.reshape(positives), mean_loss.reshape(()))
 
 
 def solution(mesh):

time: 141 us -> 138 us (0.979)
  blocking collectives: 25.3 us -> 14.5 us
  waiting for transfers between devices: 83 us -> 89.6 us
  starting transfers between devices: 3.74 us -> 7.57 us
  between operations: 3.31 us -> 0.86 us
    all_to_all x2 -> x1, blocking collectives: 25.3 us -> 14.5 us  [exchange(): return lax.all_to_all(array, 'dom', split_axis=0, concat_axis=0, tiled=True)]
    all_to_all x1 -> x2, waiting for transfers between devices: 83 us -> 89.6 us  [exchange(): return lax.all_to_all(array, 'dom', split_axis=0, concat_axis=0, tiled=True)]
    all_to_all x1 -> x2, starting transfers between devices: 3.74 us -> 7.57 us  [exchange(): return lax.all_to_all(array, 'dom', split_axis=0, concat_axis=0, tiled=True)]
    pallas_call x1 -> x2, Pallas kernels: 9.47 us -> 9.14 us  [the longest x1 8.52 us: shards(): pl.pallas_call(functools.partial(model_kernel, counts, stride, round_up(2...]
  transfers between devices with their start and end apart: 1 -> 2, of which waited for: 1 -> 2; matrix products, arithmetic and copies ran while one was open for 3% -> 3% of each run, Pallas kernels for 0% -> 0%
where the time goes in v5:
time: 138 us
  waiting for transfers between devices  89.6 us (65%)
  Pallas kernels  20.8 us (15%)
  blocking collectives  14.5 us (11%)
  starting transfers between devices  7.57 us (5%)
  local copies, waits for them, and re-layouts  2.44 us (2%)
  other arithmetic  1.71 us (1%)
    all_to_all x2, waiting for transfers between devices, exchange(): return lax.all_to_all(array, 'dom', split_axis=0, concat_axis=0, tiled=True)  89.6 us
    all_to_all x1, blocking collectives, exchange(): return lax.all_to_all(array, 'dom', split_axis=0, concat_axis=0, tiled=True)  14.5 us
    pallas_call x1, Pallas kernels, shards(): pl.pallas_call(functools.partial(gather_kernel, slots, chunk, group), out...  9.54 us
    pallas_call x1, Pallas kernels, shards(): pl.pallas_call(functools.partial(model_kernel, counts, stride, round_up(2...  8.52 us
    all_to_all x2, starting transfers between devices, exchange(): return lax.all_to_all(array, 'dom', split_axis=0, concat_axis=0, tiled=True)  7.57 us
  transfers between devices with their start and end apart: 2, of which 2 were waited for; matrix products, arithmetic and copies ran while one was open for 3% of the time, Pallas kernels for 0%

profile of v5, /device:TPU:0, one launch (start us, length us, event | category | flops | bytes accessed | tf_op | source)
XLA Modules:
  0.0 137.6 jit_solution(10170157253677381682)
XLA Ops:
  0.6 2.2 %bucket.1 = (s32[32,1,256]{2,1,0:T(1,128)S(1)}, s32[30,128]{1,0:T(8,128)S(1)}) custom-call(s32[1,288]{1,0:T(1,128)} %bitcast.17, s32[1,1152]{1,0:T(1,128)} %bitcast.16, s32[1,2304]{1,0:T(1,128)} %bitcast.15, s32[288]{0:T(512)} %refs_3_.1, s32[1152]{0:T(1024)} %refs_4_.1, s32[2304]{0:T(1024)} %refs_5_.1), custom_call_target="tpu_custom_call" | custom-call | tf_op jit(solution)/shard_map/bucket/pallas_call | solution.py:288
  2.8 14.5 %all_to_all.15.request_ref = s32[32,1,256]{2,1,0:T(1,128)} all-to-all(s32[32,1,256]{2,1,0:T(1,128)S(1)} %get-tuple-element.7), channel_id=1, replica_groups=mesh['dom'=32] {'dom'}, dimensions={0} | all-to-all | bytes 65536 | tf_op jit(solution)/shard_map/all_to_all | solution.py:269
  17.3 9.5 %owner_gather.1 = bf16[32,468,128]{2,1,0:T(8,128)(2,1)} custom-call(s32[32,1,256]{2,1,0:T(1,128)} %all_to_all.15.request_ref, bf16[16384,256]{1,0:T(8,128)(2,1)} %table_ref.1), custom_call_target="tpu_custom_call" | custom-call | tf_op jit(solution)/shard_map/owner_gather/pallas_call | solution.py:308
  26.9 0.0 copy-start.2
  26.9 0.0 copy-start.1
  26.9 3.8 %all-to-all-start.1 = ((bf16[32,468,128]{2,1,0:T(8,128)(2,1)}), bf16[32,468,128]{2,1,0:T(8,128)(2,1)}, u32[]{:S(2)}, u32[]{:S(2)}) async-start(bf16[32,468,128]{2,1,0:T(8,128)(2,1)} %owner_gather.1), calls=%async_computation.1 | async-start | bytes 7733248 | tf_op jit(solution)/shard_map/all_to_all | solution.py:269
  30.7 0.2 eq.58
  30.8 0.1 copy.28
  31.0 0.1 copy.32
  31.1 0.1 copy.29
  31.3 0.1 eq.62
  31.3 0.5 eq.68
  31.9 0.2 copy.33
  32.2 0.2 copy.37
  32.5 0.2 copy.34
  32.7 0.1 eq.72
  32.8 0.7 convert_divide_fusion.1.share1_hbm
  33.5 0.9 convert_divide_fusion.share2_hbm
  34.4 83.0 %all-to-all-done.1.got_hbm = bf16[32,468,128]{2,1,0:T(8,128)(2,1)} async-done(((bf16[32,468,128]{2,1,0:T(8,128)(2,1)}), bf16[32,468,128]{2,1,0:T(8,128)(2,1)}, u32[]{:S(2)}, u32[]{:S(2)}) %all-to-all-start.1) | async-done | bytes 3833888 | tf_op jit(solution)/shard_map/all_to_all | solution.py:269
  117.4 8.5 %model.1 = (f32[1,128]{1,0:T(1,128)S(1)}, f32[32,1,128]{2,1,0:T(1,128)}) custom-call(s32[30,128]{1,0:T(8,128)} %copy-done, bf16[32,468,128]{2,1,0:T(8,128)(2,1)} %all-to-all-done.1.got_hbm, bf16[1280,256]{1,0:T(8,128)(2,1)} %first_hbm.1, bf16[1280,256]{1,0:T(8,128)(2,1)} %second_hbm.1, f32[288,16]{1,0:T(8,128)} %convert_divide_fusion.1.share1_hbm, ...), custom_call_target="tpu_custom_call" | custom-call | tf_op jit(solution)/shard_map/model/pallas_call | solution.py:330
  125.9 3.8 %all-to-all-start.2 = ((f32[32,1,128]{2,1,0:T(1,128)}), f32[32,1,128]{2,1,0:T(1,128)S(1)}, u32[]{:S(2)}, u32[]{:S(2)}) async-start(f32[32,1,128]{2,1,0:T(1,128)} %get-tuple-element.9), calls=%async_computation.2 | async-start | bytes 32768 | tf_op jit(solution)/shard_map/all_to_all | solution.py:269
  129.8 0.5 copy.38
  130.3 6.7 %all-to-all-done.2.sums_ref = f32[32,1,128]{2,1,0:T(1,128)S(1)} async-done(((f32[32,1,128]{2,1,0:T(1,128)}), f32[32,1,128]{2,1,0:T(1,128)S(1)}, u32[]{:S(2)}, u32[]{:S(2)}) %all-to-all-start.2) | async-done | bytes 16416 | tf_op jit(solution)/shard_map/all_to_all | solution.py:269
  136.9 0.6 mean.1
  (18 shorter events, 0.2 us)
Async XLA Ops:
  2.8 24.1 %copy-start = (s32[30,128]{1,0:T(8,128)}, s32[30,128]{1,0:T(8,128)S(1)}, u32[]{:S(2)}) copy-start(s32[30,128]{1,0:T(8,128)S(1)} %get-tuple-element.6.slot_hbm) | copy-start | bytes 46084
  26.9 3.8 %copy-start.2 = (s32[1152]{0:T(1024)S(1)}, s32[1152]{0:T(1024)}, u32[]{:S(2)}) copy-start(s32[1152]{0:T(1024)} %param.19) | copy-start | bytes 13828
  26.9 4.5 %copy-start.1 = (s32[2304]{0:T(1024)S(1)}, s32[2304]{0:T(1024)}, u32[]{:S(2)}) copy-start(s32[2304]{0:T(1024)} %param.22) | copy-start | bytes 27652
  26.9 90.5 %all-to-all-start.1 = ((bf16[32,468,128]{2,1,0:T(8,128)(2,1)}), bf16[32,468,128]{2,1,0:T(8,128)(2,1)}, u32[]{:S(2)}, u32[]{:S(2)}) async-start(bf16[32,468,128]{2,1,0:T(8,128)(2,1)} %owner_gather.1), calls=%async_computation.1 | async-start | bytes 7733248 | tf_op jit(solution)/shard_map/all_to_all | solution.py:269
  125.9 11.0 %all-to-all-start.2 = ((f32[32,1,128]{2,1,0:T(1,128)}), f32[32,1,128]{2,1,0:T(1,128)S(1)}, u32[]{:S(2)}, u32[]{:S(2)}) async-start(f32[32,1,128]{2,1,0:T(1,128)} %get-tuple-element.9), calls=%async_computation.2 | async-start | bytes 32768 | tf_op jit(solution)/shard_map/all_to_all | solution.py:269

commit v6 on v5

--- a/solution.py
+++ b/solution.py
@@ -13,7 +13,7 @@
 FAN1 = 4
 FAN2 = 2
 LANES = 128
-PARTS = 4
+PARTS = 8
 HOP_STEP = 128
 F32 = jnp.float32
 BF16 = jnp.bfloat16
@@ -103,12 +103,12 @@
         lax.fori_loop(0, chunk // step, widen, 0)
     asked.wait()
 
-    def serve(device, _):
+    def serve(device):
+        turn = packed.at[device % 2]
         for slot in range(slots):
             row = pl.multiple_of(request[device, 0, slot], 2)
-            packed[pl.ds(2 * slot, 2), :] = wide[pl.ds(row, 2), :]
-        rows_out[device] = packed[: 2 * slots, :].astype(BF16)
-        return 0
+            turn[pl.ds(2 * slot, 2), :] = wide[pl.ds(row, 2), :]
+        rows_out[device] = turn[: 2 * slots, :].astype(BF16)
 
     def leave(part):
         span = pl.ds(part * group, group)
@@ -116,7 +116,7 @@
 
     for part in range(devices // group):
         for device in range(part * group, (part + 1) * group):
-            serve(device, 0)
+            serve(device)
         leave(part).start()
     for part in range(devices // group):
         leave(part).wait()
@@ -314,7 +314,7 @@
             pltpu.SMEM(arrived.shape, jnp.int32),
             pltpu.VMEM((nodes, width), BF16),
             pltpu.VMEM((2 * nodes, LANES), F32),
-            pltpu.VMEM((stride, LANES), F32),
+            pltpu.VMEM((2, stride, LANES), F32),
             pltpu.VMEM((devices, held, LANES), BF16),
             pltpu.SemaphoreType.DMA,
             pltpu.SemaphoreType.DMA((nodes // chunk,)),

time: 138 us -> 138 us (level)
  no operation moved by 1% of the time
where the time goes in v6:
time: 138 us; the launch traced here: 137 us
  waiting for transfers between devices  89.6 us (65%)
  Pallas kernels  20.7 us (15%)
  blocking collectives  14.5 us (11%)
  starting transfers between devices  7.59 us (6%)
  local copies, waits for them, and re-layouts  2.44 us (2%)
  other arithmetic  1.71 us (1%)
    all_to_all x2, waiting for transfers between devices, exchange(): return lax.all_to_all(array, 'dom', split_axis=0, concat_axis=0, tiled=True)  89.6 us
    all_to_all x1, blocking collectives, exchange(): return lax.all_to_all(array, 'dom', split_axis=0, concat_axis=0, tiled=True)  14.5 us
    pallas_call x1, Pallas kernels, shards(): pl.pallas_call(functools.partial(gather_kernel, slots, chunk, group), out...  9.42 us
    pallas_call x1, Pallas kernels, shards(): pl.pallas_call(functools.partial(model_kernel, counts, stride, round_up(2...  8.5 us
    all_to_all x2, starting transfers between devices, exchange(): return lax.all_to_all(array, 'dom', split_axis=0, concat_axis=0, tiled=True)  7.59 us
  transfers between devices with their start and end apart: 2, of which 2 were waited for; matrix products, arithmetic and copies ran while one was open for 3% of the time, Pallas kernels for 0%

profile of v6, /device:TPU:0, one launch (start us, length us, event | category | flops | bytes accessed | tf_op | source)
XLA Modules:
  0.0 137.4 jit_solution(10382443092908374474)
XLA Ops:
  0.6 2.2 %bucket.1 = (s32[32,1,256]{2,1,0:T(1,128)S(1)}, s32[30,128]{1,0:T(8,128)S(1)}) custom-call(s32[1,288]{1,0:T(1,128)} %bitcast.17, s32[1,1152]{1,0:T(1,128)} %bitcast.16, s32[1,2304]{1,0:T(1,128)} %bitcast.15, s32[288]{0:T(512)} %refs_3_.1, s32[1152]{0:T(1024)} %refs_4_.1, s32[2304]{0:T(1024)} %refs_5_.1), custom_call_target="tpu_custom_call" | custom-call | tf_op jit(solution)/shard_map/bucket/pallas_call | solution.py:288
  2.8 14.5 %all_to_all.15.request_ref = s32[32,1,256]{2,1,0:T(1,128)} all-to-all(s32[32,1,256]{2,1,0:T(1,128)S(1)} %get-tuple-element.7), channel_id=1, replica_groups=mesh['dom'=32] {'dom'}, dimensions={0} | all-to-all | bytes 65536 | tf_op jit(solution)/shard_map/all_to_all | solution.py:269
  17.3 9.4 %owner_gather.1 = bf16[32,468,128]{2,1,0:T(8,128)(2,1)} custom-call(s32[32,1,256]{2,1,0:T(1,128)} %all_to_all.15.request_ref, bf16[16384,256]{1,0:T(8,128)(2,1)} %table_ref.1), custom_call_target="tpu_custom_call" | custom-call | tf_op jit(solution)/shard_map/owner_gather/pallas_call | solution.py:308
  26.7 0.0 copy-start.2
  26.8 0.0 copy-start.1
  26.8 3.8 %all-to-all-start.1 = ((bf16[32,468,128]{2,1,0:T(8,128)(2,1)}), bf16[32,468,128]{2,1,0:T(8,128)(2,1)}, u32[]{:S(2)}, u32[]{:S(2)}) async-start(bf16[32,468,128]{2,1,0:T(8,128)(2,1)} %owner_gather.1), calls=%async_computation.1 | async-start | bytes 7733248 | tf_op jit(solution)/shard_map/all_to_all | solution.py:269
  30.5 0.2 eq.58
  30.7 0.1 copy.28
  30.9 0.1 copy.32
  31.0 0.1 copy.29
  31.1 0.1 eq.62
  31.2 0.5 eq.68
  31.8 0.2 copy.33
  32.1 0.2 copy.37
  32.4 0.2 copy.34
  32.6 0.1 eq.72
  32.7 0.7 convert_divide_fusion.1.share1_hbm
  33.4 0.9 convert_divide_fusion.share2_hbm
  34.3 83.0 %all-to-all-done.1.got_hbm = bf16[32,468,128]{2,1,0:T(8,128)(2,1)} async-done(((bf16[32,468,128]{2,1,0:T(8,128)(2,1)}), bf16[32,468,128]{2,1,0:T(8,128)(2,1)}, u32[]{:S(2)}, u32[]{:S(2)}) %all-to-all-start.1) | async-done | bytes 3833888 | tf_op jit(solution)/shard_map/all_to_all | solution.py:269
  117.3 8.5 %model.1 = (f32[1,128]{1,0:T(1,128)S(1)}, f32[32,1,128]{2,1,0:T(1,128)}) custom-call(s32[30,128]{1,0:T(8,128)} %copy-done, bf16[32,468,128]{2,1,0:T(8,128)(2,1)} %all-to-all-done.1.got_hbm, bf16[1280,256]{1,0:T(8,128)(2,1)} %first_hbm.1, bf16[1280,256]{1,0:T(8,128)(2,1)} %second_hbm.1, f32[288,16]{1,0:T(8,128)} %convert_divide_fusion.1.share1_hbm, ...), custom_call_target="tpu_custom_call" | custom-call | tf_op jit(solution)/shard_map/model/pallas_call | solution.py:330
  125.8 3.8 %all-to-all-start.2 = ((f32[32,1,128]{2,1,0:T(1,128)}), f32[32,1,128]{2,1,0:T(1,128)S(1)}, u32[]{:S(2)}, u32[]{:S(2)}) async-start(f32[32,1,128]{2,1,0:T(1,128)} %get-tuple-element.9), calls=%async_computation.2 | async-start | bytes 32768 | tf_op jit(solution)/shard_map/all_to_all | solution.py:269
  129.6 0.5 copy.38
  130.2 6.7 %all-to-all-done.2.sums_ref = f32[32,1,128]{2,1,0:T(1,128)S(1)} async-done(((f32[32,1,128]{2,1,0:T(1,128)}), f32[32,1,128]{2,1,0:T(1,128)S(1)}, u32[]{:S(2)}, u32[]{:S(2)}) %all-to-all-start.2) | async-done | bytes 16416 | tf_op jit(solution)/shard_map/all_to_all | solution.py:269
  136.8 0.6 mean.1
  (18 shorter events, 0.2 us)
Async XLA Ops:
  2.8 23.9 %copy-start = (s32[30,128]{1,0:T(8,128)}, s32[30,128]{1,0:T(8,128)S(1)}, u32[]{:S(2)}) copy-start(s32[30,128]{1,0:T(8,128)S(1)} %get-tuple-element.6.slot_hbm) | copy-start | bytes 46084
  26.7 3.8 %copy-start.2 = (s32[1152]{0:T(1024)S(1)}, s32[1152]{0:T(1024)}, u32[]{:S(2)}) copy-start(s32[1152]{0:T(1024)} %param.19) | copy-start | bytes 13828
  26.8 4.5 %copy-start.1 = (s32[2304]{0:T(1024)S(1)}, s32[2304]{0:T(1024)}, u32[]{:S(2)}) copy-start(s32[2304]{0:T(1024)} %param.22) | copy-start | bytes 27652
  26.8 90.5 %all-to-all-start.1 = ((bf16[32,468,128]{2,1,0:T(8,128)(2,1)}), bf16[32,468,128]{2,1,0:T(8,128)(2,1)}, u32[]{:S(2)}, u32[]{:S(2)}) async-start(bf16[32,468,128]{2,1,0:T(8,128)(2,1)} %owner_gather.1), calls=%async_computation.1 | async-start | bytes 7733248 | tf_op jit(solution)/shard_map/all_to_all | solution.py:269
  125.8 11.0 %all-to-all-start.2 = ((f32[32,1,128]{2,1,0:T(1,128)}), f32[32,1,128]{2,1,0:T(1,128)S(1)}, u32[]{:S(2)}, u32[]{:S(2)}) async-start(f32[32,1,128]{2,1,0:T(1,128)} %get-tuple-element.9), calls=%async_computation.2 | async-start | bytes 32768 | tf_op jit(solution)/shard_map/all_to_all | solution.py:269
